TPU v7x, 256 devices: a whole 4x4x8 slice. The times are simulated.
256 devices in a mesh: gx: 8 (over x_lo, y), gy: 4 (over x_hi, core), gz: 8 (over z).
Axes of the slice: x: 4 (x_hi: 2, x_lo: 2; x = x_hi * 2 + x_lo), y: 4, z: 8, core: 2. Of those that a mesh axis runs over, the one named last changes fastest.
Arguments:
- offsets: float32 [16, 8, 64, 16, 3], P('gx', 'gy', 'gz'), may hold values from 0.2649 to 2.3351, as said below
- velocities: float32 [16, 8, 64, 16, 3], P('gx', 'gy', 'gz'), may hold values from -6 to 6
- occupied: int32 [16, 8, 64, 16], P('gx', 'gy', 'gz'), may hold values 0 or 1
Outputs:
- positions: float32 [16, 8, 64, 16, 3], P('gx', 'gy', 'gz')
- new_velocities: float32 [16, 8, 64, 16, 3], P('gx', 'gy', 'gz')
- forces: float32 [16, 8, 64, 16, 3], P('gx', 'gy', 'gz')
- capacity_history: float32 [4, 2], replicated
Inputs may be any that keep to these rules, and one draw needn't show every extreme that they name: `offsets`: each offset lies within the cell, a jittered body-centred lattice of 16 sites with spacing 1.3 per cell, jitter at most 0.06 in each coordinate.
All inputs are finite; a program needn't handle non-finite values.
Results may differ from a plain program's by a relative error of at most 0.0003.
Values sent between devices are 32-bit elements.
A program may use at most 128 MiB of HBM per device.

v0:
```python
import jax
import jax.numpy as jnp
from jax import lax
from jax.sharding import Mesh
from jax.sharding import PartitionSpec as P

STEPS = 4
GY = ("gy_0", "gy_1")
GX = ("gx_0", "gx_1")
GX_GY_GZ = ("gx_0", "gx_1", "gy_0", "gy_1", "gz")


CUTOFF = 2.5
CELL_SIDE = 2.6
TIME_STEP = 0.005
BATH_STRENGTH = 0.25
GOAL_WARMTH = 0.8
FORCE_EDGE = 24.0 * (2.0 * CUTOFF ** (-13) - CUTOFF ** (-7))
ENERGY_EDGE = 4.0 * (CUTOFF ** (-12) - CUTOFF ** (-6))
STENCILS = [
    (along_x, along_y, along_z)
    for along_x in (-1, 0, 1)
    for along_y in (-1, 0, 1)
    for along_z in (-1, 0, 1)
]
FORWARD = [stencil for stencil in STENCILS if stencil > (0, 0, 0)]


def passed_along(block, axis, distance):
    devices = range(lax.axis_size(axis))
    route = [((i - distance) % len(devices), i) for i in devices]
    return lax.ppermute(block, axis, route)


def extended(cells, sides, width, closed):
    for axis, dim in sides:
        count = lax.axis_size(axis)
        ends = count if closed else count - 1
        head = lax.slice_in_dim(cells, 0, width, axis=dim)
        tail = lax.slice_in_dim(cells, cells.shape[dim] - width, cells.shape[dim], axis=dim)
        cells = jnp.concatenate(
            [
                lax.ppermute(tail, axis, [(i, (i + 1) % count) for i in range(ends)]),
                cells,
                lax.ppermute(head, axis, [((i + 1) % count, i) for i in range(ends)]),
            ],
            axis=dim,
        )
    return cells


def over_axes(value, axes):
    for axis in axes:
        value = lax.psum(value, axis)
    return value


def pair_terms(own_cells, neighbour, stencil):
    cell_shift = jnp.array(stencil, jnp.float32) * CELL_SIDE
    separation = neighbour[..., None, :, :3] + cell_shift - own_cells[..., :, None, :3]
    squared = jnp.sum(separation * separation, axis=-1)
    occupied_pair = own_cells[..., :, None, 3] * neighbour[..., None, :, 3]
    inside = (occupied_pair > 0.5) & (squared < CUTOFF * CUTOFF)
    if stencil == (0, 0, 0):
        slots_count = own_cells.shape[-2]
        inside = inside & jnp.logical_not(jnp.eye(slots_count, dtype=bool))
    guarded = jnp.where(inside, squared, 1.0)
    inverse = 1.0 / guarded
    inverse_six = inverse * inverse * inverse
    radius = jnp.sqrt(guarded)
    strength = (
        24.0 * (2.0 * inverse_six * inverse_six - inverse_six) * inverse - FORCE_EDGE / radius
    )
    strength = jnp.where(inside, strength, 0.0)
    energy = (
        4.0 * (inverse_six * inverse_six - inverse_six)
        - ENERGY_EDGE
        + (radius - CUTOFF) * FORCE_EDGE
    )
    energy = jnp.where(inside, energy, 0.0)
    pushes = -strength[..., None] * separation
    return (pushes, energy)


def window(padded, stencil, extent):
    return padded[
        1 + stencil[0] : 1 + stencil[0] + extent[0],
        1 + stencil[1] : 1 + stencil[1] + extent[1],
        1 + stencil[2] : 1 + stencil[2] + extent[2],
    ]


def return_ghosts(ghosted):
    depth_z = ghosted.shape[2] - 2
    from_above = passed_along(ghosted[:, :, 0], "gz", -1)
    from_below = passed_along(ghosted[:, :, depth_z + 1], "gz", 1)
    ghosted = (
        ghosted.at[:, :, depth_z].add(from_above).at[:, :, 1].add(from_below)[:, :, 1 : depth_z + 1]
    )
    height = ghosted.shape[1] - 2
    from_above = passed_along(ghosted[:, 0], GY, -1)
    from_below = passed_along(ghosted[:, height + 1], GY, 1)
    ghosted = ghosted.at[:, height].add(from_above).at[:, 1].add(from_below)[:, 1 : height + 1]
    width_x = ghosted.shape[0] - 2
    from_below = passed_along(ghosted[width_x + 1], GX, 1)
    return ghosted.at[1].add(from_below)[1 : width_x + 1]


def half_forces(padded):
    extent = (padded.shape[0] - 2, padded.shape[1] - 2, padded.shape[2] - 2)
    own_cells = window(padded, (0, 0, 0), extent)
    interior = (slice(1, 1 + extent[0]), slice(1, 1 + extent[1]), slice(1, 1 + extent[2]))
    pushes, pair_energy = pair_terms(own_cells, own_cells, (0, 0, 0))
    ghosted = jnp.zeros(padded.shape[:-1] + (3,), jnp.float32)
    ghosted = ghosted.at[interior].add(jnp.sum(pushes, axis=-2))
    energy = 0.5 * jnp.sum(pair_energy)
    for stencil in FORWARD:
        pushes, pair_energy = pair_terms(own_cells, window(padded, stencil, extent), stencil)
        target = tuple(
            (
                slice(1 + stencil[axis_id], 1 + stencil[axis_id] + extent[axis_id])
                for axis_id in range(3)
            )
        )
        ghosted = (
            ghosted.at[interior]
            .add(jnp.sum(pushes, axis=-2))
            .at[target]
            .add(-jnp.sum(pushes, axis=-3))
        )
        energy = energy + jnp.sum(pair_energy)
    return (return_ghosts(ghosted), energy)


def evaluate(position, weight):
    packed = jnp.concatenate([position, weight[..., None]], axis=-1)
    padded = extended(packed, ((GX, 0), (GY, 1), ("gz", 2)), 1, True)
    result = half_forces(padded)
    return result


def per_device(offsets, velocities, occupied):
    weight = occupied.astype(jnp.float32)
    velocity = velocities * weight[..., None]
    position = offsets
    slot_total = float(
        offsets.shape[0]
        * offsets.shape[1]
        * offsets.shape[2]
        * offsets.shape[3]
        * lax.axis_size(GX)
        * lax.axis_size(GY)
        * lax.axis_size("gz")
    )
    forces, initial_energy = evaluate(position, weight)
    records = []
    for step_index in range(STEPS):
        velocity = velocity + 0.5 * TIME_STEP * forces
        position = position + TIME_STEP * velocity
        forces, potential = evaluate(position, weight)
        velocity = velocity + 0.5 * TIME_STEP * forces
        moving_vigor = 0.5 * jnp.sum(velocity * velocity)
        moving_vigor_sum, potential_all, body_tally = (
            over_axes(moving_vigor, GX_GY_GZ),
            over_axes(potential, GX_GY_GZ),
            over_axes(jnp.sum(weight), GX_GY_GZ),
        )
        warmth_gauge = 2.0 * moving_vigor_sum / (3.0 * body_tally)
        speed_stretch = jnp.sqrt(1.0 + BATH_STRENGTH * (GOAL_WARMTH / warmth_gauge - 1.0))
        velocity = speed_stretch * velocity
        records.append(
            jnp.stack([potential_all, speed_stretch * speed_stretch * moving_vigor_sum])
            / slot_total
        )
    return (position, velocity, forces, jnp.stack(records))


def solution(mesh):
    torus = Mesh(
        mesh.devices.reshape(2, 4, 2, 2, mesh.shape["gz"]), ("gx_0", "gx_1", "gy_0", "gy_1", "gz")
    )
    in_specs = (P(GX, GY, "gz", None, None), P(GX, GY, "gz", None, None), P(GX, GY, "gz", None))
    out_specs = (
        P(GX, GY, "gz", None, None),
        P(GX, GY, "gz", None, None),
        P(GX, GY, "gz", None, None),
        P(),
    )
    return jax.shard_map(
        per_device, mesh=torus, in_specs=in_specs, out_specs=out_specs, check_vma=False
    )
```

profile of v0, /device:TPU:1, one launch (start us, length us, event | category | flops | bytes accessed | tf_op | source)
XLA Modules:
  0.0 481.6 jit_solution(9554879846550601862)
XLA Ops:
  8.2 4.4 collective-permute-start.2
  13.9 3.9 collective-permute-done.3
  19.6 4.5 collective-permute-start.4
  27.5 3.0 fusion.24
  33.0 3.0 fusion.22
  36.9 3.0 collective-permute-start.6
  41.1 4.6 collective-permute-done.7
  46.3 2.9 collective-permute-start.9
  52.8 4.1 collective-permute-done.10
  57.1 3.6 collective-permute-start.12
  62.1 4.9 %collective-permute-start.13 = (f32[4,1,8,16,4]{3,4,2,1,0:T(4,128)S(1)}, f32[4,1,8,16,4]{3,4,2,1,0:T(4,128)S(1)}, u32[]{:S(2)}, u32[]{:S(2)}) collective-permute-start(f32[4,1,8,16,4]{3,4,2,1,0:T(4,128)S(1)} %get-tuple-element.2551), channel_id=1, source_target_pairs={{0,8},{8,16},{16,24},{24,0},{1,9},{9,17},{17,25},{25,1},{2,10},{10... | collective-permute-start | bytes 24584 | tf_op jit(solution)/shard_map/ppermute | solution.py:43
  68.4 3.9 collective-permute-done.14
  77.9 2.9 fusion.50
  82.7 3.4 fusion.674
  86.0 2.9 fusion.48
  89.9 2.7 collective-permute-start.17
  93.7 3.7 collective-permute-done.18
  98.0 2.9 collective-permute-start.20
  104.4 3.8 collective-permute-done.21
  109.5 4.4 all-reduce.14
  114.0 7.8 %all-reduce.8 = (f32[]{:T(128)}, f32[]{:T(128)}) all-reduce(f32[]{:T(128)} %get-tuple-element.2345, f32[]{:T(128)} %get-tuple-element.2346), channel_id=1, replica_groups=mesh['gx_0'=2,'gx_1'=4,'gy_0'=2,'gy_1'=2,'gz'=8] {'gx_1'}, use_global_device_ids=true, to_apply=%region_43.44 | all-reduce | flops 2 | bytes 16 | tf_op jit(solution)/shard_map/psum | solution.py:54
  121.7 5.9 %all-reduce.12 = (f32[]{:T(128)}, f32[]{:T(128)}) all-reduce(f32[]{:T(128)} %get-tuple-element.2324, f32[]{:T(128)} %get-tuple-element.2325), channel_id=1, replica_groups=mesh['gx_0'=2,'gx_1'=4,'gy_0'=2,'gy_1'=2,'gz'=8] {'gy_0'}, use_global_device_ids=true, to_apply=%region_44.45 | all-reduce | flops 2 | bytes 16 | tf_op jit(solution)/shard_map/psum | solution.py:54
  127.6 9.5 %all-reduce.10 = (f32[]{:T(128)}, f32[]{:T(128)}) all-reduce(f32[]{:T(128)} %get-tuple-element.2338, f32[]{:T(128)} %get-tuple-element.2339), channel_id=1, replica_groups=mesh['gx_0'=2,'gx_1'=4,'gy_0'=2,'gy_1'=2,'gz'=8] {'gy_1'}, use_global_device_ids=true, to_apply=%region_45.46 | all-reduce | flops 2 | bytes 16 | tf_op jit(solution)/shard_map/psum | solution.py:54
  137.1 11.4 %all-reduce.6 = (f32[]{:T(128)}, f32[]{:T(128)}) all-reduce(f32[]{:T(128)} %get-tuple-element.2331, f32[]{:T(128)} %get-tuple-element.2332), channel_id=1, replica_groups=mesh['gx_0'=2,'gx_1'=4,'gy_0'=2,'gy_1'=2,'gz'=8] {'gz'}, use_global_device_ids=true, to_apply=%region_46.47 | all-reduce | flops 2 | bytes 16 | tf_op jit(solution)/shard_map/psum | solution.py:54
  150.0 3.6 collective-permute-start.23
  155.0 7.1 %collective-permute-start.24 = (f32[4,1,8,16,4]{3,4,2,1,0:T(4,128)S(1)}, f32[4,1,8,16,4]{3,4,2,1,0:T(4,128)S(1)}, u32[]{:S(2)}, u32[]{:S(2)}) collective-permute-start(f32[4,1,8,16,4]{3,4,2,1,0:T(4,128)S(1)} %get-tuple-element.2549), channel_id=1, source_target_pairs={{0,8},{8,16},{16,24},{24,0},{1,9},{9,17},{17,25},{25,1},{2,10},{10... | collective-permute-start | bytes 24584 | tf_op jit(solution)/shard_map/ppermute | solution.py:43
  163.3 3.9 collective-permute-done.25
  173.8 3.0 fusion.76
  179.9 3.1 fusion.669
  182.9 2.9 fusion.74
  190.2 3.3 collective-permute-done.29
  194.4 2.9 collective-permute-start.31
  199.0 4.8 %collective-permute-done.32 = f32[2,8,16,3]{2,3,1,0:T(4,128)S(1)} collective-permute-done((f32[2,8,16,3]{2,3,1,0:T(4,128)S(1)}, f32[2,8,16,3]{2,3,1,0:T(4,128)S(1)}, u32[]{:S(2)}, u32[]{:S(2)}) %collective-permute-start.32) | collective-permute-done | bytes 3104 | tf_op jit(solution)/shard_map/ppermute | solution.py:32
  205.1 4.3 psum.370
  209.4 7.6 %psum.371 = f32[]{:T(128)} all-reduce(f32[]{:T(128)} %psum.370), channel_id=1, replica_groups=mesh['gx_0'=2,'gx_1'=4,'gy_0'=2,'gy_1'=2,'gz'=8] {'gx_1'}, use_global_device_ids=true, to_apply=%region_137.138 | all-reduce | flops 1 | bytes 8 | tf_op jit(solution)/shard_map/psum | solution.py:54
  217.0 5.9 %psum.372 = f32[]{:T(128)} all-reduce(f32[]{:T(128)} %psum.371), channel_id=1, replica_groups=mesh['gx_0'=2,'gx_1'=4,'gy_0'=2,'gy_1'=2,'gz'=8] {'gy_0'}, use_global_device_ids=true, to_apply=%region_138.139 | all-reduce | flops 1 | bytes 8 | tf_op jit(solution)/shard_map/psum | solution.py:54
  222.9 9.2 %psum.373 = f32[]{:T(128)} all-reduce(f32[]{:T(128)} %psum.372), channel_id=1, replica_groups=mesh['gx_0'=2,'gx_1'=4,'gy_0'=2,'gy_1'=2,'gz'=8] {'gy_1'}, use_global_device_ids=true, to_apply=%region_139.140 | all-reduce | flops 1 | bytes 8 | tf_op jit(solution)/shard_map/psum | solution.py:54
  232.0 11.4 %psum.374 = f32[]{:T(128)} all-reduce(f32[]{:T(128)} %psum.373), channel_id=1, replica_groups=mesh['gx_0'=2,'gx_1'=4,'gy_0'=2,'gy_1'=2,'gz'=8] {'gz'}, use_global_device_ids=true, to_apply=%region_140.141 | all-reduce | flops 1 | bytes 8 | tf_op jit(solution)/shard_map/psum | solution.py:54
  249.2 7.2 %collective-permute-start.35 = (f32[4,1,8,16,4]{3,4,2,1,0:T(4,128)S(1)}, f32[4,1,8,16,4]{3,4,2,1,0:T(4,128)S(1)}, u32[]{:S(2)}, u32[]{:S(2)}) collective-permute-start(f32[4,1,8,16,4]{3,4,2,1,0:T(4,128)S(1)} %get-tuple-element.2547), channel_id=1, source_target_pairs={{0,8},{8,16},{16,24},{24,0},{1,9},{9,17},{17,25},{25,1},{2,10},{10... | collective-permute-start | bytes 24584 | tf_op jit(solution)/shard_map/ppermute | solution.py:43
  257.7 3.9 collective-permute-done.36
  267.8 2.9 fusion.102
  272.8 3.3 fusion.744
  276.1 2.9 fusion.100
  283.3 3.7 collective-permute-done.40
  287.6 3.4 collective-permute-start.42
  292.3 4.8 %collective-permute-done.43 = f32[2,8,16,3]{2,3,1,0:T(4,128)S(1)} collective-permute-done((f32[2,8,16,3]{2,3,1,0:T(4,128)S(1)}, f32[2,8,16,3]{2,3,1,0:T(4,128)S(1)}, u32[]{:S(2)}, u32[]{:S(2)}) %collective-permute-start.43) | collective-permute-done | bytes 3104 | tf_op jit(solution)/shard_map/ppermute | solution.py:32
  298.4 4.4 psum.375
  302.8 8.2 %psum.376 = f32[]{:T(128)} all-reduce(f32[]{:T(128)} %psum.375), channel_id=1, replica_groups=mesh['gx_0'=2,'gx_1'=4,'gy_0'=2,'gy_1'=2,'gz'=8] {'gx_1'}, use_global_device_ids=true, to_apply=%region_184.185 | all-reduce | flops 1 | bytes 8 | tf_op jit(solution)/shard_map/psum | solution.py:54
  311.0 6.0 %psum.377 = f32[]{:T(128)} all-reduce(f32[]{:T(128)} %psum.376), channel_id=1, replica_groups=mesh['gx_0'=2,'gx_1'=4,'gy_0'=2,'gy_1'=2,'gz'=8] {'gy_0'}, use_global_device_ids=true, to_apply=%region_185.186 | all-reduce | flops 1 | bytes 8 | tf_op jit(solution)/shard_map/psum | solution.py:54
  317.0 10.3 %psum.378 = f32[]{:T(128)} all-reduce(f32[]{:T(128)} %psum.377), channel_id=1, replica_groups=mesh['gx_0'=2,'gx_1'=4,'gy_0'=2,'gy_1'=2,'gz'=8] {'gy_1'}, use_global_device_ids=true, to_apply=%region_186.187 | all-reduce | flops 1 | bytes 8 | tf_op jit(solution)/shard_map/psum | solution.py:54
  327.3 11.5 %psum.379 = f32[]{:T(128)} all-reduce(f32[]{:T(128)} %psum.378), channel_id=1, replica_groups=mesh['gx_0'=2,'gx_1'=4,'gy_0'=2,'gy_1'=2,'gz'=8] {'gz'}, use_global_device_ids=true, to_apply=%region_187.188 | all-reduce | flops 1 | bytes 8 | tf_op jit(solution)/shard_map/psum | solution.py:54
  340.3 3.6 collective-permute-start.45
  345.2 7.1 %collective-permute-start.46 = (f32[4,1,8,16,4]{3,4,2,1,0:T(4,128)S(1)}, f32[4,1,8,16,4]{3,4,2,1,0:T(4,128)S(1)}, u32[]{:S(2)}, u32[]{:S(2)}) collective-permute-start(f32[4,1,8,16,4]{3,4,2,1,0:T(4,128)S(1)} %get-tuple-element.2545), channel_id=1, source_target_pairs={{0,8},{8,16},{16,24},{24,0},{1,9},{9,17},{17,25},{25,1},{2,10},{10... | collective-permute-start | bytes 24584 | tf_op jit(solution)/shard_map/ppermute | solution.py:43
  353.7 3.9 collective-permute-done.47
  365.1 2.9 fusion.609
  368.4 3.1 fusion.128
  372.5 3.3 fusion.884
  380.4 2.9 fusion.126
  387.8 3.3 collective-permute-done.51
  435.5 4.4 all-reduce.13
  439.9 9.3 %all-reduce.7 = (f32[]{:T(128)}, f32[]{:T(128)}, f32[]{:T(128)}, f32[]{:T(128)}, f32[]{:T(128)}) all-reduce(f32[]{:T(128)} %get-tuple-element.2340, f32[]{:T(128)} %get-tuple-element.2341, f32[]{:T(128)} %get-tuple-element.2342, f32[]{:T(128)} %get-tuple-element.2343, ...), channel_id=1, replica_groups=mesh['gx_0'=2,'gx_1'=4,'gy_0'=2,'gy_1'=2,'gz'=8] {'gx_1'}, use_global_device_ids=true, to_apply=%region_231.232 | all-reduce | flops 5 | bytes 40 | tf_op jit(solution)/shard_map/psum | solution.py:54
  449.2 6.0 %all-reduce.11 = (f32[]{:T(128)}, f32[]{:T(128)}, f32[]{:T(128)}, f32[]{:T(128)}, f32[]{:T(128)}) all-reduce(f32[]{:T(128)} %get-tuple-element.2319, f32[]{:T(128)} %get-tuple-element.2320, f32[]{:T(128)} %get-tuple-element.2321, f32[]{:T(128)} %get-tuple-element.2322, ...), channel_id=1, replica_groups=mesh['gx_0'=2,'gx_1'=4,'gy_0'=2,'gy_1'=2,'gz'=8] {'gy_0'}, use_global_device_ids=true, to_apply=%region_232.233 | all-reduce | flops 5 | bytes 40 | tf_op jit(solution)/shard_map/psum | solution.py:54
  455.1 8.9 %all-reduce.9 = (f32[]{:T(128)}, f32[]{:T(128)}, f32[]{:T(128)}, f32[]{:T(128)}, f32[]{:T(128)}) all-reduce(f32[]{:T(128)} %get-tuple-element.2333, f32[]{:T(128)} %get-tuple-element.2334, f32[]{:T(128)} %get-tuple-element.2335, f32[]{:T(128)} %get-tuple-element.2336, ...), channel_id=1, replica_groups=mesh['gx_0'=2,'gx_1'=4,'gy_0'=2,'gy_1'=2,'gz'=8] {'gy_1'}, use_global_device_ids=true, to_apply=%region_233.234 | all-reduce | flops 5 | bytes 40 | tf_op jit(solution)/shard_map/psum | solution.py:54
  464.1 11.5 %all-reduce.5 = (f32[]{:T(128)}, f32[1,1]{0,1:T(1,128)}, f32[1,1]{0,1:T(1,128)}, f32[1,1]{0,1:T(1,128)}, f32[1,1]{0,1:T(1,128)}) all-reduce(f32[]{:T(128)} %get-tuple-element.2326, f32[1,1]{0,1:T(1,128)} %bitcast.126, f32[1,1]{0,1:T(1,128)} %bitcast.124, ...), channel_id=1, replica_groups=mesh['gx_0'=2,'gx_1'=4,'gy_0'=2,'gy_1'=2,'gz'=8] {'gz'}, use_global_device_ids=true, to_apply=%region_234.235 | all-reduce | flops 5 | bytes 40 | tf_op jit(solution)/shard_map/psum | solution.py:54
  (514 shorter events, 112.9 us)
Async XLA Ops:
  2.2 5.9 %collective-permute-start = (f32[1,2,8,16,4]{3,4,2,1,0:T(4,128)S(1)}, f32[1,2,8,16,4]{3,4,2,1,0:T(4,128)S(1)}, u32[]{:S(2)}, u32[]{:S(2)}) collective-permute-start(f32[1,2,8,16,4]{3,4,2,1,0:T(4,128)S(1)} %get-tuple-element.2563), channel_id=1, source_target_pairs={{0,32},{32,64},{64,96},{96,128},{128,160},{160,192},{192,224},{224... | collective-permute-start | bytes 12296 | tf_op jit(solution)/shard_map/ppermute | solution.py:43
  4.4 3.7 collective-permute-start.1
  6.9 260.4 %copy-start.21 = (pred[16,16]{1,0:T(8,128)(4,1)}, pred[16,16]{1,0:T(8,128)(4,1)S(1)}, u32[]{:S(2)}) copy-start(pred[16,16]{1,0:T(8,128)(4,1)S(1)} %fusion.1173) | copy-start | bytes 772
  8.2 5.8 %collective-permute-start.2 = (f32[4,1,8,16,4]{3,4,2,1,0:T(4,128)S(1)}, f32[4,1,8,16,4]{3,4,2,1,0:T(4,128)S(1)}, u32[]{:S(2)}, u32[]{:S(2)}) collective-permute-start(f32[4,1,8,16,4]{3,4,2,1,0:T(4,128)S(1)} %get-tuple-element.2553), channel_id=1, source_target_pairs={{0,8},{8,16},{16,24},{24,0},{1,9},{9,17},{17,25},{25,1},{2,10},{10... | collective-permute-start | bytes 24584 | tf_op jit(solution)/shard_map/ppermute | solution.py:43
  12.6 5.2 %collective-permute-start.3 = (f32[4,1,8,16,4]{3,4,2,1,0:T(4,128)S(1)}, f32[4,1,8,16,4]{3,4,2,1,0:T(4,128)S(1)}, u32[]{:S(2)}, u32[]{:S(2)}) collective-permute-start(f32[4,1,8,16,4]{3,4,2,1,0:T(4,128)S(1)} %get-tuple-element.2554), channel_id=1, source_target_pairs={{8,0},{16,8},{24,16},{0,24},{9,1},{17,9},{25,17},{1,25},{10,2},{18... | collective-permute-start | bytes 24584 | tf_op jit(solution)/shard_map/ppermute | solution.py:45
  17.9 7.2 %collective-permute-start.5 = (f32[4,4,1,16,4]{3,4,2,1,0:T(4,128)S(1)}, f32[4,4,1,16,4]{3,4,2,1,0:T(4,128)S(1)}, u32[]{:S(2)}, u32[]{:S(2)}) collective-permute-start(f32[4,4,1,16,4]{3,4,2,1,0:T(4,128)S(1)} %get-tuple-element.2511), channel_id=1, source_target_pairs={{0,1},{1,2},{2,3},{3,4},{4,5},{5,6},{6,7},{7,0},{8,9},{9,10},{10,1... | collective-permute-start | bytes 12296 | tf_op jit(solution)/shard_map/ppermute | solution.py:43
  19.6 5.5 %collective-permute-start.4 = (f32[4,4,1,16,4]{3,4,2,1,0:T(4,128)S(1)}, f32[4,4,1,16,4]{3,4,2,1,0:T(4,128)S(1)}, u32[]{:S(2)}, u32[]{:S(2)}) collective-permute-start(f32[4,4,1,16,4]{3,4,2,1,0:T(4,128)S(1)} %get-tuple-element.2512), channel_id=1, source_target_pairs={{1,0},{2,1},{3,2},{4,3},{5,4},{6,5},{7,6},{0,7},{9,8},{10,9},{11,1... | collective-permute-start | bytes 12296 | tf_op jit(solution)/shard_map/ppermute | solution.py:45
  36.9 4.1 collective-permute-start.6
  41.0 4.7 collective-permute-start.7
  45.8 5.9 %collective-permute-start.8 = (f32[4,8,16,3]{2,1,3,0:T(8,128)S(1)}, f32[4,8,16,3]{2,1,3,0:T(8,128)S(1)}, u32[]{:S(2)}, u32[]{:S(2)}) collective-permute-start(f32[4,8,16,3]{2,1,3,0:T(8,128)S(1)} %bitcast.330), channel_id=1, source_target_pairs={{8,0},{16,8},{24,16},{0,24},{9,1},{17,9},{25,17},{1,25},{10,2},{18... | collective-permute-start | bytes 18440 | tf_op jit(solution)/shard_map/ppermute | solution.py:32
  46.3 5.4 %collective-permute-start.9 = (f32[4,8,16,3]{2,1,3,0:T(8,128)S(1)}, f32[4,8,16,3]{2,1,3,0:T(8,128)S(1)}, u32[]{:S(2)}, u32[]{:S(2)}) collective-permute-start(f32[4,8,16,3]{2,1,3,0:T(8,128)S(1)} %bitcast.331), channel_id=1, source_target_pairs={{24,0},{0,8},{8,16},{16,24},{25,1},{1,9},{9,17},{17,25},{26,2},{2,... | collective-permute-start | bytes 18440 | tf_op jit(solution)/shard_map/ppermute | solution.py:32
  51.8 5.1 %collective-permute-start.10 = (f32[2,8,16,3]{2,3,1,0:T(4,128)S(1)}, f32[2,8,16,3]{2,3,1,0:T(4,128)S(1)}, u32[]{:S(2)}, u32[]{:S(2)}) collective-permute-start(f32[2,8,16,3]{2,3,1,0:T(4,128)S(1)} %slice_bitcast_fusion.16), channel_id=1, source_target_pairs={{224,0},{0,32},{32,64},{64,96},{96,128},{128,160},{160,192},{192,2... | collective-permute-start | bytes 9224 | tf_op jit(solution)/shard_map/ppermute | solution.py:32
  52.8 4.1 copy-start.11
  52.8 4.1 copy-start.12
  57.0 5.0 %collective-permute-start.11 = (f32[1,2,8,16,4]{3,4,2,1,0:T(4,128)S(1)}, f32[1,2,8,16,4]{3,4,2,1,0:T(4,128)S(1)}, u32[]{:S(2)}, u32[]{:S(2)}) collective-permute-start(f32[1,2,8,16,4]{3,4,2,1,0:T(4,128)S(1)} %get-tuple-element.2561), channel_id=1, source_target_pairs={{0,32},{32,64},{64,96},{96,128},{128,160},{160,192},{192,224},{224... | collective-permute-start | bytes 12296 | tf_op jit(solution)/shard_map/ppermute | solution.py:43
  57.1 4.9 %collective-permute-start.12 = (f32[1,2,8,16,4]{3,4,2,1,0:T(4,128)S(1)}, f32[1,2,8,16,4]{3,4,2,1,0:T(4,128)S(1)}, u32[]{:S(2)}, u32[]{:S(2)}) collective-permute-start(f32[1,2,8,16,4]{3,4,2,1,0:T(4,128)S(1)} %get-tuple-element.2562), channel_id=1, source_target_pairs={{32,0},{64,32},{96,64},{128,96},{160,128},{192,160},{224,192},{0,2... | collective-permute-start | bytes 12296 | tf_op jit(solution)/shard_map/ppermute | solution.py:45
  62.1 6.3 %collective-permute-start.13 = (f32[4,1,8,16,4]{3,4,2,1,0:T(4,128)S(1)}, f32[4,1,8,16,4]{3,4,2,1,0:T(4,128)S(1)}, u32[]{:S(2)}, u32[]{:S(2)}) collective-permute-start(f32[4,1,8,16,4]{3,4,2,1,0:T(4,128)S(1)} %get-tuple-element.2551), channel_id=1, source_target_pairs={{0,8},{8,16},{16,24},{24,0},{1,9},{9,17},{17,25},{25,1},{2,10},{10... | collective-permute-start | bytes 24584 | tf_op jit(solution)/shard_map/ppermute | solution.py:43
  67.0 5.2 %collective-permute-start.14 = (f32[4,1,8,16,4]{3,4,2,1,0:T(4,128)S(1)}, f32[4,1,8,16,4]{3,4,2,1,0:T(4,128)S(1)}, u32[]{:S(2)}, u32[]{:S(2)}) collective-permute-start(f32[4,1,8,16,4]{3,4,2,1,0:T(4,128)S(1)} %get-tuple-element.2552), channel_id=1, source_target_pairs={{8,0},{16,8},{24,16},{0,24},{9,1},{17,9},{25,17},{1,25},{10,2},{18... | collective-permute-start | bytes 24584 | tf_op jit(solution)/shard_map/ppermute | solution.py:45
  72.3 4.1 collective-permute-start.16
  72.4 4.0 collective-permute-start.15
  89.9 3.8 collective-permute-start.17
  92.7 4.7 collective-permute-start.18
  97.4 5.5 %collective-permute-start.19 = (f32[4,8,16,3]{2,1,3,0:T(8,128)S(1)}, f32[4,8,16,3]{2,1,3,0:T(8,128)S(1)}, u32[]{:S(2)}, u32[]{:S(2)}) collective-permute-start(f32[4,8,16,3]{2,1,3,0:T(8,128)S(1)} %bitcast.332), channel_id=1, source_target_pairs={{8,0},{16,8},{24,16},{0,24},{9,1},{17,9},{25,17},{1,25},{10,2},{18... | collective-permute-start | bytes 18440 | tf_op jit(solution)/shard_map/ppermute | solution.py:32
  98.0 5.0 %collective-permute-start.20 = (f32[4,8,16,3]{2,1,3,0:T(8,128)S(1)}, f32[4,8,16,3]{2,1,3,0:T(8,128)S(1)}, u32[]{:S(2)}, u32[]{:S(2)}) collective-permute-start(f32[4,8,16,3]{2,1,3,0:T(8,128)S(1)} %bitcast.333), channel_id=1, source_target_pairs={{24,0},{0,8},{8,16},{16,24},{25,1},{1,9},{9,17},{17,25},{26,2},{2,... | collective-permute-start | bytes 18440 | tf_op jit(solution)/shard_map/ppermute | solution.py:32
  103.0 5.2 %collective-permute-start.21 = (f32[2,8,16,3]{2,3,1,0:T(4,128)S(1)}, f32[2,8,16,3]{2,3,1,0:T(4,128)S(1)}, u32[]{:S(2)}, u32[]{:S(2)}) collective-permute-start(f32[2,8,16,3]{2,3,1,0:T(4,128)S(1)} %slice_bitcast_fusion.12), channel_id=1, source_target_pairs={{224,0},{0,32},{32,64},{64,96},{96,128},{128,160},{160,192},{192,2... | collective-permute-start | bytes 9224 | tf_op jit(solution)/shard_map/ppermute | solution.py:32
  149.9 5.0 %collective-permute-start.22 = (f32[1,2,8,16,4]{3,4,2,1,0:T(4,128)S(1)}, f32[1,2,8,16,4]{3,4,2,1,0:T(4,128)S(1)}, u32[]{:S(2)}, u32[]{:S(2)}) collective-permute-start(f32[1,2,8,16,4]{3,4,2,1,0:T(4,128)S(1)} %get-tuple-element.2559), channel_id=1, source_target_pairs={{0,32},{32,64},{64,96},{96,128},{128,160},{160,192},{192,224},{224... | collective-permute-start | bytes 12296 | tf_op jit(solution)/shard_map/ppermute | solution.py:43
  150.0 4.9 %collective-permute-start.23 = (f32[1,2,8,16,4]{3,4,2,1,0:T(4,128)S(1)}, f32[1,2,8,16,4]{3,4,2,1,0:T(4,128)S(1)}, u32[]{:S(2)}, u32[]{:S(2)}) collective-permute-start(f32[1,2,8,16,4]{3,4,2,1,0:T(4,128)S(1)} %get-tuple-element.2560), channel_id=1, source_target_pairs={{32,0},{64,32},{96,64},{128,96},{160,128},{192,160},{224,192},{0,2... | collective-permute-start | bytes 12296 | tf_op jit(solution)/shard_map/ppermute | solution.py:45
  155.0 8.4 %collective-permute-start.24 = (f32[4,1,8,16,4]{3,4,2,1,0:T(4,128)S(1)}, f32[4,1,8,16,4]{3,4,2,1,0:T(4,128)S(1)}, u32[]{:S(2)}, u32[]{:S(2)}) collective-permute-start(f32[4,1,8,16,4]{3,4,2,1,0:T(4,128)S(1)} %get-tuple-element.2549), channel_id=1, source_target_pairs={{0,8},{8,16},{16,24},{24,0},{1,9},{9,17},{17,25},{25,1},{2,10},{10... | collective-permute-start | bytes 24584 | tf_op jit(solution)/shard_map/ppermute | solution.py:43
  162.0 5.2 %collective-permute-start.25 = (f32[4,1,8,16,4]{3,4,2,1,0:T(4,128)S(1)}, f32[4,1,8,16,4]{3,4,2,1,0:T(4,128)S(1)}, u32[]{:S(2)}, u32[]{:S(2)}) collective-permute-start(f32[4,1,8,16,4]{3,4,2,1,0:T(4,128)S(1)} %get-tuple-element.2550), channel_id=1, source_target_pairs={{8,0},{16,8},{24,16},{0,24},{9,1},{17,9},{25,17},{1,25},{10,2},{18... | collective-permute-start | bytes 24584 | tf_op jit(solution)/shard_map/ppermute | solution.py:45
  167.3 4.1 collective-permute-start.27
  169.1 3.1 collective-permute-start.26
  172.5 4.5 copy-start.13
  172.5 4.5 copy-start.15
  176.8 2.1 copy-start.8
  186.8 3.4 collective-permute-start.28
  189.1 4.5 collective-permute-start.29
  193.6 5.1 %collective-permute-start.30 = (f32[4,8,16,3]{2,1,3,0:T(8,128)S(1)}, f32[4,8,16,3]{2,1,3,0:T(8,128)S(1)}, u32[]{:S(2)}, u32[]{:S(2)}) collective-permute-start(f32[4,8,16,3]{2,1,3,0:T(8,128)S(1)} %bitcast.334), channel_id=1, source_target_pairs={{8,0},{16,8},{24,16},{0,24},{9,1},{17,9},{25,17},{1,25},{10,2},{18... | collective-permute-start | bytes 18440 | tf_op jit(solution)/shard_map/ppermute | solution.py:32
  194.4 4.3 collective-permute-start.31
  198.8 5.0 %collective-permute-start.32 = (f32[2,8,16,3]{2,3,1,0:T(4,128)S(1)}, f32[2,8,16,3]{2,3,1,0:T(4,128)S(1)}, u32[]{:S(2)}, u32[]{:S(2)}) collective-permute-start(f32[2,8,16,3]{2,3,1,0:T(4,128)S(1)} %slice_bitcast_fusion.8), channel_id=1, source_target_pairs={{224,0},{0,32},{32,64},{64,96},{96,128},{128,160},{160,192},{192,2... | collective-permute-start | bytes 9224 | tf_op jit(solution)/shard_map/ppermute | solution.py:32
  244.1 5.0 %collective-permute-start.33 = (f32[1,2,8,16,4]{3,4,2,1,0:T(4,128)S(1)}, f32[1,2,8,16,4]{3,4,2,1,0:T(4,128)S(1)}, u32[]{:S(2)}, u32[]{:S(2)}) collective-permute-start(f32[1,2,8,16,4]{3,4,2,1,0:T(4,128)S(1)} %get-tuple-element.2557), channel_id=1, source_target_pairs={{0,32},{32,64},{64,96},{96,128},{128,160},{160,192},{192,224},{224... | collective-permute-start | bytes 12296 | tf_op jit(solution)/shard_map/ppermute | solution.py:43
  245.4 3.7 collective-permute-start.34
  249.2 8.5 %collective-permute-start.35 = (f32[4,1,8,16,4]{3,4,2,1,0:T(4,128)S(1)}, f32[4,1,8,16,4]{3,4,2,1,0:T(4,128)S(1)}, u32[]{:S(2)}, u32[]{:S(2)}) collective-permute-start(f32[4,1,8,16,4]{3,4,2,1,0:T(4,128)S(1)} %get-tuple-element.2547), channel_id=1, source_target_pairs={{0,8},{8,16},{16,24},{24,0},{1,9},{9,17},{17,25},{25,1},{2,10},{10... | collective-permute-start | bytes 24584 | tf_op jit(solution)/shard_map/ppermute | solution.py:43
  256.3 5.2 %collective-permute-start.36 = (f32[4,1,8,16,4]{3,4,2,1,0:T(4,128)S(1)}, f32[4,1,8,16,4]{3,4,2,1,0:T(4,128)S(1)}, u32[]{:S(2)}, u32[]{:S(2)}) collective-permute-start(f32[4,1,8,16,4]{3,4,2,1,0:T(4,128)S(1)} %get-tuple-element.2548), channel_id=1, source_target_pairs={{8,0},{16,8},{24,16},{0,24},{9,1},{17,9},{25,17},{1,25},{10,2},{18... | collective-permute-start | bytes 24584 | tf_op jit(solution)/shard_map/ppermute | solution.py:45
  261.6 4.1 collective-permute-start.38
  263.3 3.0 collective-permute-start.37
  266.5 4.4 copy-start.17
  266.5 4.4 copy-start.19
  279.9 3.4 collective-permute-start.39
  282.3 4.6 collective-permute-start.40
  287.0 5.1 %collective-permute-start.41 = (f32[4,8,16,3]{2,1,3,0:T(8,128)S(1)}, f32[4,8,16,3]{2,1,3,0:T(8,128)S(1)}, u32[]{:S(2)}, u32[]{:S(2)}) collective-permute-start(f32[4,8,16,3]{2,1,3,0:T(8,128)S(1)} %bitcast.336), channel_id=1, source_target_pairs={{8,0},{16,8},{24,16},{0,24},{9,1},{17,9},{25,17},{1,25},{10,2},{18... | collective-permute-start | bytes 18440 | tf_op jit(solution)/shard_map/ppermute | solution.py:32
  287.6 4.6 collective-permute-start.42
  292.2 5.0 %collective-permute-start.43 = (f32[2,8,16,3]{2,3,1,0:T(4,128)S(1)}, f32[2,8,16,3]{2,3,1,0:T(4,128)S(1)}, u32[]{:S(2)}, u32[]{:S(2)}) collective-permute-start(f32[2,8,16,3]{2,3,1,0:T(4,128)S(1)} %slice_bitcast_fusion.4), channel_id=1, source_target_pairs={{224,0},{0,32},{32,64},{64,96},{96,128},{128,160},{160,192},{192,2... | collective-permute-start | bytes 9224 | tf_op jit(solution)/shard_map/ppermute | solution.py:32
  340.2 5.0 %collective-permute-start.44 = (f32[1,2,8,16,4]{3,4,2,1,0:T(4,128)S(1)}, f32[1,2,8,16,4]{3,4,2,1,0:T(4,128)S(1)}, u32[]{:S(2)}, u32[]{:S(2)}) collective-permute-start(f32[1,2,8,16,4]{3,4,2,1,0:T(4,128)S(1)} %get-tuple-element.2555), channel_id=1, source_target_pairs={{0,32},{32,64},{64,96},{96,128},{128,160},{160,192},{192,224},{224... | collective-permute-start | bytes 12296 | tf_op jit(solution)/shard_map/ppermute | solution.py:43
  340.3 4.9 %collective-permute-start.45 = (f32[1,2,8,16,4]{3,4,2,1,0:T(4,128)S(1)}, f32[1,2,8,16,4]{3,4,2,1,0:T(4,128)S(1)}, u32[]{:S(2)}, u32[]{:S(2)}) collective-permute-start(f32[1,2,8,16,4]{3,4,2,1,0:T(4,128)S(1)} %get-tuple-element.2556), channel_id=1, source_target_pairs={{32,0},{64,32},{96,64},{128,96},{160,128},{192,160},{224,192},{0,2... | collective-permute-start | bytes 12296 | tf_op jit(solution)/shard_map/ppermute | solution.py:45
  345.2 8.4 %collective-permute-start.46 = (f32[4,1,8,16,4]{3,4,2,1,0:T(4,128)S(1)}, f32[4,1,8,16,4]{3,4,2,1,0:T(4,128)S(1)}, u32[]{:S(2)}, u32[]{:S(2)}) collective-permute-start(f32[4,1,8,16,4]{3,4,2,1,0:T(4,128)S(1)} %get-tuple-element.2545), channel_id=1, source_target_pairs={{0,8},{8,16},{16,24},{24,0},{1,9},{9,17},{17,25},{25,1},{2,10},{10... | collective-permute-start | bytes 24584 | tf_op jit(solution)/shard_map/ppermute | solution.py:43
  352.3 5.2 %collective-permute-start.47 = (f32[4,1,8,16,4]{3,4,2,1,0:T(4,128)S(1)}, f32[4,1,8,16,4]{3,4,2,1,0:T(4,128)S(1)}, u32[]{:S(2)}, u32[]{:S(2)}) collective-permute-start(f32[4,1,8,16,4]{3,4,2,1,0:T(4,128)S(1)} %get-tuple-element.2546), channel_id=1, source_target_pairs={{8,0},{16,8},{24,16},{0,24},{9,1},{17,9},{25,17},{1,25},{10,2},{18... | collective-permute-start | bytes 24584 | tf_op jit(solution)/shard_map/ppermute | solution.py:45
  357.6 4.4 collective-permute-start.49
  359.1 2.9 collective-permute-start.48
  363.9 1.2 copy-start.7
  384.2 3.5 collective-permute-start.50
  386.6 4.5 collective-permute-start.51
  391.2 20.9 %collective-permute-start.52 = (f32[4,8,16,3]{2,1,3,0:T(8,128)S(1)}, f32[4,8,16,3]{2,1,3,0:T(8,128)S(1)}, u32[]{:S(2)}, u32[]{:S(2)}) collective-permute-start(f32[4,8,16,3]{2,1,3,0:T(8,128)S(1)} %bitcast.329), channel_id=1, source_target_pairs={{8,0},{16,8},{24,16},{0,24},{9,1},{17,9},{25,17},{1,25},{10,2},{18... | collective-permute-start | bytes 18440 | tf_op jit(solution)/shard_map/ppermute | solution.py:32
  409.4 3.9 collective-permute-start.53
  413.3 19.4 %collective-permute-start.54 = (f32[2,8,16,3]{2,3,1,0:T(4,128)S(1)}, f32[2,8,16,3]{2,3,1,0:T(4,128)S(1)}, u32[]{:S(2)}, u32[]{:S(2)}) collective-permute-start(f32[2,8,16,3]{2,3,1,0:T(4,128)S(1)} %slice_bitcast_fusion), channel_id=1, source_target_pairs={{224,0},{0,32},{32,64},{64,96},{96,128},{128,160},{160,192},{192,2... | collective-permute-start | bytes 9224 | tf_op jit(solution)/shard_map/ppermute | solution.py:32
  (39 other events, 28.5 us)
where the time goes:
time: 490 us; the launch traced here: 482 us
  blocking collectives  158 us (32%)
  starting transfers between devices  100 us (20%)
  waiting for transfers between devices  83.4 us (17%)
  other arithmetic  80.9 us (17%)
  between operations  46.3 us (9%)
  local copies, waits for them, and re-layouts  13.4 us (3%)
    psum x20, blocking collectives, over_axes(): value = lax.psum(value, axis)  158 us
    ppermute x25, waiting for transfers between devices, passed_along(): return lax.ppermute(block, axis, route)  49.2 us
    ppermute x15, starting transfers between devices, extended(): lax.ppermute(tail, axis, [(i, (i + 1) % count) for i in range(ends)])  41.3 us
    reduce_sum x15, other arithmetic, half_forces(): jnp.sum(pushes, axis=-3)  34.5 us
    ppermute x25, starting transfers between devices, passed_along(): return lax.ppermute(block, axis, route)  32.3 us
    ppermute x15, starting transfers between devices, extended(): lax.ppermute(head, axis, [((i + 1) % count, i) for i in range(ends)])  26.5 us
    ppermute x15, waiting for transfers between devices, extended(): lax.ppermute(head, axis, [((i + 1) % count, i) for i in range(ends)])  20.9 us
    reduce_sum x6, other arithmetic, half_forces(): energy = energy + jnp.sum(pair_energy)  16.7 us
  transfers between devices with their start and end apart: 55, of which 39 were waited for; matrix products, arithmetic and copies ran while one was open for 1% of the time, Pallas kernels for 0%

commit v1 on v0

v1 whole, which is shorter than its diff:
```python
import functools
import itertools

import jax
import jax.numpy as jnp
from jax import lax
from jax.experimental import pallas as pl
from jax.experimental.pallas import tpu as pltpu
from jax.sharding import PartitionSpec as P

STEPS = 4
ROUNDS = STEPS + 1
CUTOFF = 2.5
CELL_SIDE = 2.6
TIME_STEP = 0.005
BATH_STRENGTH = 0.25
GOAL_WARMTH = 0.8
FORCE_EDGE = 24.0 * (2.0 * CUTOFF ** (-13) - CUTOFF ** (-7))
ENERGY_EDGE = 4.0 * (CUTOFF ** (-12) - CUTOFF ** (-6))
ENERGY_SHIFT = -ENERGY_EDGE - CUTOFF * FORCE_EDGE
FAR = 1.0e6
MESH = pl.DeviceIdType.MESH
LANES = 128
SLOTS = 16
DEPTH = 8

SIDES = {0: (pl.ds(0, 2), pl.ds(1, 2)), 1: (pl.ds(1, 1), pl.ds(0, 1)), -1: (pl.ds(0, 1), pl.ds(3, 1))}
NEIGHBOURS = sorted(
    (d for d in itertools.product((-1, 0, 1), repeat=3) if d != (0, 0, 0)),
    key=lambda d: -(2 * abs(d[0]) + 2 * abs(d[1]) + abs(d[2])),
)


def lane_take(x, lanes):
    return jnp.take_along_axis(x, lanes, axis=1, mode="promise_in_bounds")


def kernel(
    sizes, o_ref, v_ref, w_ref, oo_ref, vo_ref, fo_ref, hist_ref,
    buf, zsrc, zbuf, red_a, red_b, expand, acc, state, shifted, strip,
    halo_recv, halo_send, z_recv, z_send, a_recv, a_send, b_recv, b_send,
):
    nx, ny, nz = sizes
    gx, gy, gz = (lax.axis_index(a) for a in ("gx", "gy", "gz"))
    high, core = gy // 2, gy % 2
    n_high = ny // 2

    def at(dx, dy, dz):
        return (lax.rem(gx + dx + nx, nx), lax.rem(gy + dy + ny, ny), lax.rem(gz + dz + nz, nz))

    group_a = [
        (gx, high * 2 + lax.rem(core + dc, 2), lax.rem(gz + dz, nz))
        for dz in range(nz) for dc in range(2) if (dz, dc) != (0, 0)
    ]
    me_a = gz * 2 + core
    group_b = [
        (lax.rem(gx + dx, nx), lax.rem(high + dh, n_high) * 2 + core, gz)
        for dx in range(nx) for dh in range(n_high) if (dx, dh) != (0, 0)
    ]
    me_b = gx * n_high + high
    size_a, size_b = nz * 2, nx * n_high

    barrier = pltpu.get_barrier_semaphore()
    peers = [at(*d) for d in NEIGHBOURS] + group_a + group_b
    for peer in peers:
        pl.semaphore_signal(barrier, inc=1, device_id=peer, device_id_type=MESH)

    lane = lax.broadcasted_iota(jnp.int32, (8, LANES), 1)
    row = lax.broadcasted_iota(jnp.int32, (8, LANES), 0)
    slot, cell = lane % SLOTS, lane // SLOTS
    lane1 = lane[:1]

    def flatten(block):
        strip[:, :SLOTS] = block
        spread = lane_take(strip[...], slot)
        return jnp.sum(jnp.where(cell == row, spread, 0.0), axis=0, keepdims=True)

    for k in range(16):
        state[k] = jnp.zeros((8, LANES), jnp.float32)
    POS, VEL, FORCE, BASE, TERM, WEIGHT = 0, 3, 6, 9, 12, 15
    for c in range(4):
        cx, cy = c // 2, c % 2
        state[WEIGHT, c : c + 1, :] = flatten(w_ref[cx, cy].astype(jnp.float32))
        for k in range(3):
            state[BASE + k, c : c + 1, :] = flatten(o_ref[cx, cy, k])
            state[VEL + k, c : c + 1, :] = flatten(v_ref[cx, cy, k])
    for k in range(3):
        state[VEL + k] = state[VEL + k] * state[WEIGHT]
    acc[...] = jnp.zeros_like(acc)
    for r in range(ROUNDS):
        for cx in range(2):
            for cy in range(2):
                buf[r, 1 + cx, 1 + cy] = jnp.zeros((2, 4, LANES), jnp.float32)

    def ship(r):
        here = state[WEIGHT] > 0.5
        base = [jnp.where(here, state[BASE + k], FAR) for k in range(3)]
        term = [state[TERM + k] for k in range(3)]
        for c in range(4):
            for k in range(3):
                buf[r, 1 + c // 2, 1 + c % 2, 0, k : k + 1, :] = base[k][c : c + 1]
                buf[r, 1 + c // 2, 1 + c % 2, 1, k : k + 1, :] = term[k][c : c + 1]
        for end in range(2):
            pick = slot + end * (LANES - SLOTS)
            packed = jnp.zeros((8, LANES), jnp.float32)
            for k in range(3):
                packed = jnp.where(cell == k + 4 * end, lane_take(base[k], pick), packed)
                packed = jnp.where(cell == k + 4 - 4 * end, lane_take(term[k], pick), packed)
            for c in range(4):
                zsrc[r, end, c // 2, c % 2] = packed[c : c + 1]
        for dx, dy, dz in NEIGHBOURS:
            (from_x, to_x), (from_y, to_y) = SIDES[dx], SIDES[dy]
            if dz == 0:
                own_x, own_y = pl.ds(from_x.start + 1, from_x.size), pl.ds(from_y.start + 1, from_y.size)
                pltpu.make_async_remote_copy(
                    src_ref=buf.at[r, own_x, own_y], dst_ref=buf.at[r, to_x, to_y],
                    send_sem=halo_send.at[r], recv_sem=halo_recv.at[r],
                    device_id=at(dx, dy, dz), device_id_type=MESH,
                ).start()
            else:
                end = 0 if dz < 0 else 1
                pltpu.make_async_remote_copy(
                    src_ref=zsrc.at[r, end, from_x, from_y], dst_ref=zbuf.at[r, end, to_x, to_y],
                    send_sem=z_send.at[r], recv_sem=z_recv.at[r],
                    device_id=at(dx, dy, dz), device_id_type=MESH,
                ).start()

    def all_of(ref, sem):
        pltpu.make_async_copy(ref, ref, sem).wait()

    def share(stage, me, group, send_sem, recv_sem, k, value):
        stage[k, me] = value
        for peer in group:
            pltpu.make_async_remote_copy(
                src_ref=stage.at[k, me], dst_ref=stage.at[k, me],
                send_sem=send_sem.at[k], recv_sem=recv_sem.at[k],
                device_id=peer, device_id_type=MESH,
            ).start()

    def collect(stage, size, recv_sem, k):
        all_of(stage.at[k, pl.ds(0, size - 1)], recv_sem.at[k])
        return jnp.sum(stage[k], axis=0)

    def half_sum(value, width):
        while width < LANES:
            value = value + pltpu.roll(value, width, 1)
            width *= 2
        return value

    count = jnp.sum(state[WEIGHT], axis=0, keepdims=True)
    count = count + pltpu.roll(count, 64, 1)
    count = count + pltpu.roll(count, 32, 1)

    pl.semaphore_wait(barrier, len(peers))
    ship(0)

    def one_round(r, stretch):
        wide = jnp.broadcast_to(stretch, (8, LANES))
        half_step = jnp.where(r == 0, 0.0, 0.5 * TIME_STEP)
        here = state[WEIGHT] > 0.5
        position, velocity = [], []
        for k in range(3):
            position.append(state[BASE + k] + wide * state[TERM + k])
            velocity.append(wide * state[VEL + k] + (0.5 * TIME_STEP) * state[FORCE + k])
            state[POS + k] = position[k]
            for dz in (-1, 0, 1):
                moved = pltpu.roll(position[k], (SLOTS * dz) % LANES, 1) if dz else position[k]
                shifted[dz + 1, k] = moved - CELL_SIDE * dz if k == 2 else moved

        all_of(buf.at[r, pl.ds(0, 3)], halo_recv.at[r])
        all_of(zbuf.at[r], z_recv.at[r])

        narrow = wide[:1]
        spread_lanes = [cell * SLOTS + row + 8 * h for h in range(2)]
        for x in range(4):
            for y in range(4):
                col = buf[r, x, y, 0] + wide[:4] * buf[r, x, y, 1]
                ends = [zbuf[r, e, x, y] for e in range(2)]
                ends = [e + narrow * pltpu.roll(e, 64, 1) for e in ends]
                ends = jnp.where(lane1 < 64, ends[0], ends[1])
                ends = jnp.broadcast_to(ends, (8, LANES))
                for k in range(3):
                    line = jnp.broadcast_to(col[k : k + 1], (8, LANES))
                    for h in range(2):
                        level = lane_take(line, spread_lanes[h])
                        end_lanes = jnp.where(lane < 64, 0, 64) + (k * SLOTS + 8 * h) + row
                        ghost = lane_take(ends, end_lanes)
                        expand[x * 4 + y, 0, k, h] = jnp.where(cell == DEPTH - 1, ghost, level)
                        expand[x * 4 + y, 1, k, h] = level
                        expand[x * 4 + y, 2, k, h] = jnp.where(cell == 0, ghost, level)

        def one_column(c, carry):
            base = (c // 2) * 4 + c % 2
            total = [None] * 4
            for dz in (-1, 0, 1):
                own = [jnp.broadcast_to(shifted[dz + 1, k, pl.ds(c, 1), :], (8, LANES)) for k in range(3)]
                part = [jnp.zeros((8, LANES), jnp.float32)] * 4
                for dx in (-1, 0, 1):
                    own_x = own[0] - CELL_SIDE * dx
                    for dy in (-1, 0, 1):
                        own_y = own[1] - CELL_SIDE * dy
                        other = base + (dx + 1) * 4 + dy + 1
                        for h in range(2):
                            sx = expand[other, dz + 1, 0, h] - own_x
                            sy = expand[other, dz + 1, 1, h] - own_y
                            sz = expand[other, dz + 1, 2, h] - own[2]
                            squared = sx * sx + sy * sy + sz * sz
                            inside = squared < CUTOFF * CUTOFF
                            if (dx, dy, dz) == (0, 0, 0):
                                inside = inside & (slot != row + 8 * h)
                                squared = jnp.where(inside, squared, 1.0)
                            inverse_root = lax.rsqrt(squared)
                            inverse = inverse_root * inverse_root
                            six = inverse * inverse * inverse
                            strength = (48.0 * six - 24.0) * six * inverse - FORCE_EDGE * inverse_root
                            strength = jnp.where(inside, strength, 0.0)
                            energy = (six - 1.0) * six * 4.0 + (squared * inverse_root * FORCE_EDGE + ENERGY_SHIFT)
                            energy = jnp.where(inside, energy, 0.0)
                            part[0] = part[0] - strength * sx
                            part[1] = part[1] - strength * sy
                            part[2] = part[2] - strength * sz
                            part[3] = part[3] + energy
                for k in range(4):
                    back = pltpu.roll(part[k], (-SLOTS * dz) % LANES, 1) if dz else part[k]
                    total[k] = back if total[k] is None else total[k] + back
            for k in range(4):
                acc[k, c] = total[k]
            return carry

        lax.fori_loop(0, 4, one_column, 0)

        sums = []
        for k in range(4):
            for c in range(4):
                strip[c : c + 1, :] = jnp.sum(acc[k, c], axis=0, keepdims=True)
            sums.append(jnp.where(here & (row < 4), strip[...], 0.0))
        force, energy = sums[:3], sums[3]
        vigor = jnp.zeros((8, LANES), jnp.float32)
        for k in range(3):
            velocity[k] = velocity[k] + half_step * force[k]
            vigor = vigor + velocity[k] * velocity[k]

        @pl.when(r > 0)
        def _():
            k_row = half_sum(jnp.sum(vigor, axis=0, keepdims=True), 64)
            u_row = half_sum(jnp.sum(energy, axis=0, keepdims=True), 32)
            n_row = count
            value = jnp.where(lane1 < 64, k_row, jnp.where(lane1 < 96, u_row, n_row))
            share(red_a, me_a, group_a, a_send, a_recv, r - 1, value)

        for k in range(3):
            state[VEL + k] = velocity[k]
            state[FORCE + k] = force[k]
            state[BASE + k] = position[k] + (0.5 * TIME_STEP * TIME_STEP) * force[k]
            state[TERM + k] = TIME_STEP * velocity[k]

        @pl.when(r < STEPS)
        def _():
            ship(r + 1)

        def reduced():
            value = collect(red_a, size_a, a_recv, r - 1)
            share(red_b, me_b, group_b, b_send, b_recv, r - 1, value)
            value = collect(red_b, size_b, b_recv, r - 1)
            vigor_sum = 0.5 * jnp.sum(jnp.where(lane1 < 64, value, 0.0), axis=1, keepdims=True)
            body_tally = jnp.sum(jnp.where(lane1 >= 96, value, 0.0), axis=1, keepdims=True)
            potential = 0.5 * jnp.sum(jnp.where((lane1 >= 64) & (lane1 < 96), value, 0.0), axis=1, keepdims=True)
            warmth = 2.0 * vigor_sum / (3.0 * body_tally)
            new = jnp.sqrt(1.0 + BATH_STRENGTH * (GOAL_WARMTH / warmth - 1.0))
            slot_total = float(nx * ny * nz * 4 * DEPTH * SLOTS)
            record = jnp.where(row == 0, potential, new * new * vigor_sum) / slot_total
            acc[4, 0] = jnp.where(lane == r - 1, record, acc[4, 0])
            return new

        return lax.cond(r > 0, reduced, lambda: jnp.ones((1, 1), jnp.float32))

    stretch = lax.fori_loop(0, ROUNDS, one_round, jnp.ones((1, 1), jnp.float32))

    def unflatten(line):
        lanes = row * SLOTS + slot
        return lane_take(jnp.broadcast_to(line, (8, LANES)), lanes)[:, :SLOTS]

    for c in range(4):
        for k in range(3):
            oo_ref[c // 2, c % 2, k] = unflatten(state[POS + k, c : c + 1, :])
            vo_ref[c // 2, c % 2, k] = unflatten(stretch * state[VEL + k, c : c + 1, :])
            fo_ref[c // 2, c % 2, k] = unflatten(state[FORCE + k, c : c + 1, :])
    hist_ref[...] = acc[4, 0][:2, :STEPS]

    def drain(r, carry):
        all_of(buf.at[r, pl.ds(0, 3)], halo_send.at[r])
        all_of(zbuf.at[r], z_send.at[r])
        return carry

    lax.fori_loop(0, ROUNDS, drain, 0)

    def drain_sums(k, carry):
        all_of(red_a.at[k, pl.ds(0, size_a - 1)], a_send.at[k])
        all_of(red_b.at[k, pl.ds(0, size_b - 1)], b_send.at[k])
        return carry

    lax.fori_loop(0, STEPS, drain_sums, 0)


def per_device(sizes, offsets, velocities, occupied):
    nx, ny, nz = sizes
    size_a, size_b = nz * 2, nx * (ny // 2)
    order = (0, 1, 4, 2, 3)
    block = jax.ShapeDtypeStruct((2, 2, 3, DEPTH, SLOTS), jnp.float32)
    whole = pl.BlockSpec(memory_space=pltpu.VMEM)
    dma = pltpu.SemaphoreType.DMA
    vmem = functools.partial(lambda *shape: pltpu.VMEM(shape, jnp.float32))
    position, velocity, force, history = pl.pallas_call(
        functools.partial(kernel, sizes),
        out_shape=(block, block, block, jax.ShapeDtypeStruct((2, STEPS), jnp.float32)),
        in_specs=[whole] * 3,
        out_specs=(whole,) * 4,
        scratch_shapes=[
            vmem(ROUNDS, 4, 4, 2, 4, LANES),
            vmem(ROUNDS, 2, 2, 2, 1, LANES),
            vmem(ROUNDS, 2, 4, 4, 1, LANES),
            vmem(STEPS, size_a, 1, LANES),
            vmem(STEPS, size_b, 1, LANES),
            vmem(16, 3, 3, 2, 8, LANES),
            vmem(5, 4, 8, LANES),
            vmem(16, 8, LANES),
            vmem(3, 3, 8, LANES),
            vmem(8, LANES),
            dma((ROUNDS,)), dma((ROUNDS,)), dma((ROUNDS,)), dma((ROUNDS,)),
            dma((STEPS,)), dma((STEPS,)), dma((STEPS,)), dma((STEPS,)),
        ],
        compiler_params=pltpu.CompilerParams(collective_id=0, has_side_effects=True),
        name="window",
    )(offsets.transpose(order), velocities.transpose(order), occupied)
    back = (0, 1, 3, 4, 2)
    return (position.transpose(back), velocity.transpose(back), force.transpose(back), history.T)


def solution(mesh):
    sizes = tuple(mesh.shape[a] for a in ("gx", "gy", "gz"))
    cells = P("gx", "gy", "gz", None, None)
    return jax.shard_map(
        functools.partial(per_device, sizes),
        mesh=mesh,
        in_specs=(cells, cells, P("gx", "gy", "gz", None)),
        out_specs=(cells, cells, cells, P()),
        check_vma=False,
    )
```

time: 490 us -> 77 us (0.16); the launches traced: 482 us -> 76.8 us
  blocking collectives: 158 us -> 0 us
  starting transfers between devices: 100 us -> 0 us
  waiting for transfers between devices: 83.4 us -> 0 us
  other arithmetic: 80.9 us -> 0 us
  Pallas kernels: 0 us -> 72.7 us
  between operations: 46.3 us -> 0.65 us
  local copies, waits for them, and re-layouts: 13.4 us -> 3.44 us
    psum x20 -> x0, blocking collectives: 158 us -> none  [over_axes(): value = lax.psum(value, axis)]
    ppermute x55 -> x0, starting transfers between devices: 100 us -> none  [the longest x15 41.3 us: extended(): lax.ppermute(tail, axis, [(i, (i + 1) % count) for i in range(ends)])]
    ppermute x55 -> x0, waiting for transfers between devices: 83.4 us -> none  [the longest x25 49.2 us: passed_along(): return lax.ppermute(block, axis, route)]
    pallas_call x0 -> x1, Pallas kernels: none -> 72.7 us  [per_device(): pl.pallas_call(functools.partial(kernel, sizes), out_shape=(block, block,...]
    reduce_sum x31 -> x0, other arithmetic: 58.8 us -> none  [the longest x15 34.5 us: half_forces(): jnp.sum(pushes, axis=-3)]
    unnamed x100 -> x10, local copies, waits for them, and re-layouts: 11.1 us -> 3.44 us
    neg x10 -> x0, other arithmetic: 6.84 us -> none  [pair_terms(): pushes = -strength[..., None] * separation]
    scatter-add x150 -> x0, other arithmetic: 5.3 us -> none  [the longest x126 4.64 us: half_forces(): ghosted = ghosted.at[interior].add(jnp.sum(pushes, axis=-2)).at[target].a...]
  transfers between devices with their start and end apart: 55 -> 0, of which waited for: 39 -> 0; matrix products, arithmetic and copies ran while one was open for 1% -> 0% of each run, Pallas kernels for 0% -> 0%
where the time goes in v1:
time: 77 us; the launch traced here: 76.8 us
  Pallas kernels  72.7 us (94%)
  local copies, waits for them, and re-layouts  3.44 us (4%)
    pallas_call x1, Pallas kernels, per_device(): pl.pallas_call(functools.partial(kernel, sizes), out_shape=(block, block,...  72.7 us
    unnamed x10, local copies, waits for them, and re-layouts  3.44 us

profile of v1, /device:TPU:1, one launch (start us, length us, event | category | flops | bytes accessed | tf_op | source)
XLA Modules:
  0.0 76.8 jit_solution(13093703437310117200)
XLA Ops:
  0.6 72.7 %window.1 = (f32[2,2,3,8,16]{4,3,2,1,0:T(8,128)}, f32[2,2,3,8,16]{4,3,2,1,0:T(8,128)}, f32[2,2,3,8,16]{4,3,2,1,0:T(8,128)}, f32[2,4]{1,0:T(2,128)}) custom-call(f32[2,2,3,8,16]{4,3,2,1,0:T(8,128)} %bitcast.6, f32[2,2,3,8,16]{4,3,2,1,0:T(8,128)} %bitcast.7, s32[2,2,8,16]{3,2,1,0:T(8,128)} %w_ref.1), custom_call_target="tpu_custom_call" | custom-call | tf_op jit(solution)/shard_map/window/pallas_call | solution.py:313
  73.3 0.0 copy-start.1
  73.3 1.4 %copy.11 = f32[2,2,8,16,3]{3,2,4,1,0:T(8,128)} copy(f32[2,2,8,16,3]{3,2,4,1,0:T(8,128)} %bitcast.10) | data formatting | bytes 12288
  74.8 0.0 copy-done.1
  74.8 0.0 copy-start
  74.8 0.6 copy.12
  75.4 0.2 copy-done
  75.6 0.0 copy-start.2
  75.6 0.6 copy.13
  76.2 0.0 copy-done.2
  76.2 0.6 copy.14
Async XLA Ops:
  73.3 1.4 %copy-start.1 = (f32[2,2,3,8,16]{4,3,2,1,0:T(8,128)S(1)}, f32[2,2,3,8,16]{4,3,2,1,0:T(8,128)}, u32[]{:S(2)}) copy-start(f32[2,2,3,8,16]{4,3,2,1,0:T(8,128)} %get-tuple-element.9) | copy-start | bytes 18436
  74.8 0.8 %copy-start = (f32[2,2,3,8,16]{4,3,2,1,0:T(8,128)S(1)}, f32[2,2,3,8,16]{4,3,2,1,0:T(8,128)}, u32[]{:S(2)}) copy-start(f32[2,2,3,8,16]{4,3,2,1,0:T(8,128)} %get-tuple-element.10) | copy-start | bytes 18436
  75.6 0.6 copy-start.2

commit v2 on v1

--- a/solution.py
+++ b/solution.py
@@ -36,7 +36,7 @@
 
 
 def kernel(
-    sizes, o_ref, v_ref, w_ref, oo_ref, vo_ref, fo_ref, hist_ref,
+    sizes, o_ref, v_ref, w_ref, out_ref,
     buf, zsrc, zbuf, red_a, red_b, expand, acc, state, shifted, strip,
     halo_recv, halo_send, z_recv, z_send, a_recv, a_send, b_recv, b_send,
 ):
@@ -276,16 +276,11 @@
 
     stretch = lax.fori_loop(0, ROUNDS, one_round, jnp.ones((1, 1), jnp.float32))
 
-    def unflatten(line):
-        lanes = row * SLOTS + slot
-        return lane_take(jnp.broadcast_to(line, (8, LANES)), lanes)[:, :SLOTS]
-
-    for c in range(4):
-        for k in range(3):
-            oo_ref[c // 2, c % 2, k] = unflatten(state[POS + k, c : c + 1, :])
-            vo_ref[c // 2, c % 2, k] = unflatten(stretch * state[VEL + k, c : c + 1, :])
-            fo_ref[c // 2, c % 2, k] = unflatten(state[FORCE + k, c : c + 1, :])
-    hist_ref[...] = acc[4, 0][:2, :STEPS]
+    for k in range(3):
+        out_ref[k] = state[POS + k]
+        out_ref[3 + k] = stretch * state[VEL + k]
+        out_ref[6 + k] = state[FORCE + k]
+    out_ref[9] = acc[4, 0]
 
     def drain(r, carry):
         all_of(buf.at[r, pl.ds(0, 3)], halo_send.at[r])
@@ -300,6 +295,18 @@
         return carry
 
     lax.fori_loop(0, STEPS, drain_sums, 0)
+
+
+def unfold(in_ref, oo_ref, vo_ref, fo_ref, hist_ref):
+    lane = lax.broadcasted_iota(jnp.int32, (8, LANES), 1)
+    row = lax.broadcasted_iota(jnp.int32, (8, LANES), 0)
+    lanes = row * SLOTS + lane % SLOTS
+    for n, ref in enumerate((oo_ref, vo_ref, fo_ref)):
+        for k in range(3):
+            for c in range(4):
+                line = jnp.broadcast_to(in_ref[3 * n + k, c : c + 1, :], (8, LANES))
+                ref[c // 2, c % 2, k] = lane_take(line, lanes)[:, :SLOTS]
+    hist_ref[...] = in_ref[9, :2, :STEPS]
 
 
 def per_device(sizes, offsets, velocities, occupied):
@@ -310,11 +317,11 @@
     whole = pl.BlockSpec(memory_space=pltpu.VMEM)
     dma = pltpu.SemaphoreType.DMA
     vmem = functools.partial(lambda *shape: pltpu.VMEM(shape, jnp.float32))
-    position, velocity, force, history = pl.pallas_call(
+    lines = pl.pallas_call(
         functools.partial(kernel, sizes),
-        out_shape=(block, block, block, jax.ShapeDtypeStruct((2, STEPS), jnp.float32)),
+        out_shape=pltpu.VMEM((10, 8, LANES), jnp.float32),
         in_specs=[whole] * 3,
-        out_specs=(whole,) * 4,
+        out_specs=whole,
         scratch_shapes=[
             vmem(ROUNDS, 4, 4, 2, 4, LANES),
             vmem(ROUNDS, 2, 2, 2, 1, LANES),
@@ -332,6 +339,13 @@
         compiler_params=pltpu.CompilerParams(collective_id=0, has_side_effects=True),
         name="window",
     )(offsets.transpose(order), velocities.transpose(order), occupied)
+    position, velocity, force, history = pl.pallas_call(
+        unfold,
+        out_shape=(block, block, block, jax.ShapeDtypeStruct((2, STEPS), jnp.float32)),
+        in_specs=[whole],
+        out_specs=(whole,) * 4,
+        name="unfold",
+    )(pltpu.with_memory_space_constraint(lines, pltpu.VMEM))
     back = (0, 1, 3, 4, 2)
     return (position.transpose(back), velocity.transpose(back), force.transpose(back), history.T)
 

time: 77 us -> 73.4 us (0.953)
  local copies, waits for them, and re-layouts: 3.44 us -> 0 us
    unnamed x10 -> x0, local copies, waits for them, and re-layouts: 3.44 us -> none
    pallas_call x1 -> x2, Pallas kernels: 72.7 us -> 72.7 us  [the longest x1 71.9 us: per_device(): pl.pallas_call(functools.partial(kernel, sizes), out_shape=pltpu.VMEM((10...]
where the time goes in v2:
time: 73.4 us; the launch traced here: 73.3 us
  Pallas kernels  72.7 us (99%)
    pallas_call x1, Pallas kernels, per_device(): pl.pallas_call(functools.partial(kernel, sizes), out_shape=pltpu.VMEM((10...  71.9 us

profile of v2, /device:TPU:1, one launch (start us, length us, event | category | flops | bytes accessed | tf_op | source)
XLA Modules:
  0.0 73.3 jit_solution(15007701334051051718)
XLA Ops:
  0.6 71.9 %window.1.in_ref = f32[10,8,128]{2,1,0:T(8,128)S(1)} custom-call(f32[2,2,3,8,16]{4,3,2,1,0:T(8,128)} %bitcast.6, f32[2,2,3,8,16]{4,3,2,1,0:T(8,128)} %bitcast.7, s32[2,2,8,16]{3,2,1,0:T(8,128)} %w_ref.1), custom_call_target="tpu_custom_call" | custom-call | tf_op jit(solution)/shard_map/window/pallas_call | solution.py:320
  72.6 0.7 %unfold.1 = (f32[2,2,3,8,16]{4,3,2,1,0:T(8,128)}, f32[2,2,3,8,16]{4,3,2,1,0:T(8,128)}, f32[2,2,3,8,16]{4,3,2,1,0:T(8,128)}, f32[2,4]{1,0:T(2,128)}) custom-call(f32[10,8,128]{2,1,0:T(8,128)S(1)} %window.1.in_ref), custom_call_target="tpu_custom_call" | custom-call | tf_op jit(solution)/shard_map/unfold/pallas_call | solution.py:342

commit v3 on v2

--- a/solution.py
+++ b/solution.py
@@ -18,6 +18,9 @@
 FORCE_EDGE = 24.0 * (2.0 * CUTOFF ** (-13) - CUTOFF ** (-7))
 ENERGY_EDGE = 4.0 * (CUTOFF ** (-12) - CUTOFF ** (-6))
 ENERGY_SHIFT = -ENERGY_EDGE - CUTOFF * FORCE_EDGE
+UNIT = 2.0 ** (1.0 / 6.0)
+SIDE = CELL_SIDE / UNIT
+EDGE = FORCE_EDGE * UNIT / 12.0
 FAR = 1.0e6
 MESH = pl.DeviceIdType.MESH
 LANES = 128
@@ -36,8 +39,8 @@
 
 
 def kernel(
-    sizes, o_ref, v_ref, w_ref, out_ref,
-    buf, zsrc, zbuf, red_a, red_b, expand, acc, state, shifted, strip,
+    sizes, o_hbm, v_hbm, w_hbm, out_ref, o_ref, v_ref, w_ref, in_sem,
+    buf, zsrc, zbuf, red_a, red_b, lines, expand, acc, state, shifted, strip,
     halo_recv, halo_send, z_recv, z_send, a_recv, a_send, b_recv, b_send,
 ):
     nx, ny, nz = sizes
@@ -65,25 +68,34 @@
     for peer in peers:
         pl.semaphore_signal(barrier, inc=1, device_id=peer, device_id_type=MESH)
 
+    fetches = [
+        pltpu.make_async_copy(src, dst, in_sem.at[n])
+        for n, (src, dst) in enumerate(((o_hbm, o_ref), (v_hbm, v_ref), (w_hbm, w_ref)))
+    ]
+    for fetch in fetches:
+        fetch.start()
+
     lane = lax.broadcasted_iota(jnp.int32, (8, LANES), 1)
     row = lax.broadcasted_iota(jnp.int32, (8, LANES), 0)
     slot, cell = lane % SLOTS, lane // SLOTS
     lane1 = lane[:1]
 
-    def flatten(block):
-        strip[:, :SLOTS] = block
-        spread = lane_take(strip[...], slot)
+    def flatten(n, block):
+        expand[n // 18, n // 6 % 3, n // 2 % 3, n % 2, :, :SLOTS] = block
+        spread = lane_take(expand[n // 18, n // 6 % 3, n // 2 % 3, n % 2], slot)
         return jnp.sum(jnp.where(cell == row, spread, 0.0), axis=0, keepdims=True)
 
     for k in range(16):
         state[k] = jnp.zeros((8, LANES), jnp.float32)
     POS, VEL, FORCE, BASE, TERM, WEIGHT = 0, 3, 6, 9, 12, 15
+    for fetch in fetches:
+        fetch.wait()
     for c in range(4):
         cx, cy = c // 2, c % 2
-        state[WEIGHT, c : c + 1, :] = flatten(w_ref[cx, cy].astype(jnp.float32))
-        for k in range(3):
-            state[BASE + k, c : c + 1, :] = flatten(o_ref[cx, cy, k])
-            state[VEL + k, c : c + 1, :] = flatten(v_ref[cx, cy, k])
+        state[WEIGHT, c : c + 1, :] = flatten(7 * c, w_ref[cx, cy].astype(jnp.float32))
+        for k in range(3):
+            state[BASE + k, c : c + 1, :] = flatten(7 * c + 1 + k, o_ref[cx, cy, k])
+            state[VEL + k, c : c + 1, :] = flatten(7 * c + 4 + k, v_ref[cx, cy, k])
     for k in range(3):
         state[VEL + k] = state[VEL + k] * state[WEIGHT]
     acc[...] = jnp.zeros_like(acc)
@@ -104,8 +116,9 @@
             pick = slot + end * (LANES - SLOTS)
             packed = jnp.zeros((8, LANES), jnp.float32)
             for k in range(3):
-                packed = jnp.where(cell == k + 4 * end, lane_take(base[k], pick), packed)
-                packed = jnp.where(cell == k + 4 - 4 * end, lane_take(term[k], pick), packed)
+                place = (2 * k + (DEPTH - 1) * end) % DEPTH
+                packed = jnp.where(cell == place, lane_take(base[k], pick), packed)
+                packed = jnp.where(cell == (place + 1) % DEPTH, lane_take(term[k], pick), packed)
             for c in range(4):
                 zsrc[r, end, c // 2, c % 2] = packed[c : c + 1]
         for dx, dy, dz in NEIGHBOURS:
@@ -164,30 +177,34 @@
             velocity.append(wide * state[VEL + k] + (0.5 * TIME_STEP) * state[FORCE + k])
             state[POS + k] = position[k]
             for dz in (-1, 0, 1):
-                moved = pltpu.roll(position[k], (SLOTS * dz) % LANES, 1) if dz else position[k]
-                shifted[dz + 1, k] = moved - CELL_SIDE * dz if k == 2 else moved
+                moved = position[k] * (1.0 / UNIT)
+                moved = pltpu.roll(moved, (SLOTS * dz) % LANES, 1) if dz else moved
+                shifted[dz + 1, k] = moved - SIDE * dz if k == 2 else moved
 
         all_of(buf.at[r, pl.ds(0, 3)], halo_recv.at[r])
         all_of(zbuf.at[r], z_recv.at[r])
 
         narrow = wide[:1]
-        spread_lanes = [cell * SLOTS + row + 8 * h for h in range(2)]
         for x in range(4):
             for y in range(4):
-                col = buf[r, x, y, 0] + wide[:4] * buf[r, x, y, 1]
+                lines[x * 4 + y, 0] = (buf[r, x, y, 0] + wide[:4] * buf[r, x, y, 1]) * (1.0 / UNIT)
                 ends = [zbuf[r, e, x, y] for e in range(2)]
-                ends = [e + narrow * pltpu.roll(e, 64, 1) for e in ends]
-                ends = jnp.where(lane1 < 64, ends[0], ends[1])
-                ends = jnp.broadcast_to(ends, (8, LANES))
+                ends = [e + narrow * pltpu.roll(e, LANES - SLOTS, 1) for e in ends]
+                ends = jnp.where(cell[:1] % 2 == 0, ends[0], ends[1]) * (1.0 / UNIT)
                 for k in range(3):
-                    line = jnp.broadcast_to(col[k : k + 1], (8, LANES))
-                    for h in range(2):
-                        level = lane_take(line, spread_lanes[h])
-                        end_lanes = jnp.where(lane < 64, 0, 64) + (k * SLOTS + 8 * h) + row
-                        ghost = lane_take(ends, end_lanes)
-                        expand[x * 4 + y, 0, k, h] = jnp.where(cell == DEPTH - 1, ghost, level)
-                        expand[x * 4 + y, 1, k, h] = level
-                        expand[x * 4 + y, 2, k, h] = jnp.where(cell == 0, ghost, level)
+                    turned = pltpu.roll(ends, LANES - 2 * SLOTS * k, 1) if k else ends
+                    lines[x * 4 + y, 1, k : k + 1, :] = turned
+        for h in range(2):
+            spread_lanes = cell * SLOTS + row + 8 * h
+            for n in range(16):
+                for k in range(3):
+                    level, ghost = (
+                        lane_take(jnp.broadcast_to(lines[n, e, k : k + 1, :], (8, LANES)), spread_lanes)
+                        for e in range(2)
+                    )
+                    expand[n, 0, k, h] = jnp.where(cell == DEPTH - 1, ghost, level)
+                    expand[n, 1, k, h] = level
+                    expand[n, 2, k, h] = jnp.where(cell == 0, ghost, level)
 
         def one_column(c, carry):
             base = (c // 2) * 4 + c % 2
@@ -196,30 +213,29 @@
                 own = [jnp.broadcast_to(shifted[dz + 1, k, pl.ds(c, 1), :], (8, LANES)) for k in range(3)]
                 part = [jnp.zeros((8, LANES), jnp.float32)] * 4
                 for dx in (-1, 0, 1):
-                    own_x = own[0] - CELL_SIDE * dx
+                    own_x = own[0] - SIDE * dx
                     for dy in (-1, 0, 1):
-                        own_y = own[1] - CELL_SIDE * dy
+                        own_y = own[1] - SIDE * dy
                         other = base + (dx + 1) * 4 + dy + 1
                         for h in range(2):
                             sx = expand[other, dz + 1, 0, h] - own_x
                             sy = expand[other, dz + 1, 1, h] - own_y
                             sz = expand[other, dz + 1, 2, h] - own[2]
                             squared = sx * sx + sy * sy + sz * sz
-                            inside = squared < CUTOFF * CUTOFF
+                            inside = squared < (CUTOFF / UNIT) ** 2
                             if (dx, dy, dz) == (0, 0, 0):
                                 inside = inside & (slot != row + 8 * h)
                                 squared = jnp.where(inside, squared, 1.0)
                             inverse_root = lax.rsqrt(squared)
                             inverse = inverse_root * inverse_root
                             six = inverse * inverse * inverse
-                            strength = (48.0 * six - 24.0) * six * inverse - FORCE_EDGE * inverse_root
-                            strength = jnp.where(inside, strength, 0.0)
-                            energy = (six - 1.0) * six * 4.0 + (squared * inverse_root * FORCE_EDGE + ENERGY_SHIFT)
-                            energy = jnp.where(inside, energy, 0.0)
-                            part[0] = part[0] - strength * sx
-                            part[1] = part[1] - strength * sy
-                            part[2] = part[2] - strength * sz
-                            part[3] = part[3] + energy
+                            wall = six * (six - 1.0)
+                            strength = jnp.where(inside, wall * inverse - EDGE * inverse_root, 0.0)
+                            energy = (wall - six) + (squared * inverse_root * (12.0 * EDGE) + ENERGY_SHIFT)
+                            part[0] = part[0] + strength * sx
+                            part[1] = part[1] + strength * sy
+                            part[2] = part[2] + strength * sz
+                            part[3] = part[3] + jnp.where(inside, energy, 0.0)
                 for k in range(4):
                     back = pltpu.roll(part[k], (-SLOTS * dz) % LANES, 1) if dz else part[k]
                     total[k] = back if total[k] is None else total[k] + back
@@ -234,7 +250,7 @@
             for c in range(4):
                 strip[c : c + 1, :] = jnp.sum(acc[k, c], axis=0, keepdims=True)
             sums.append(jnp.where(here & (row < 4), strip[...], 0.0))
-        force, energy = sums[:3], sums[3]
+        force, energy = [total * (-12.0 / UNIT) for total in sums[:3]], sums[3]
         vigor = jnp.zeros((8, LANES), jnp.float32)
         for k in range(3):
             velocity[k] = velocity[k] + half_step * force[k]
@@ -320,14 +336,16 @@
     lines = pl.pallas_call(
         functools.partial(kernel, sizes),
         out_shape=pltpu.VMEM((10, 8, LANES), jnp.float32),
-        in_specs=[whole] * 3,
+        in_specs=[pl.BlockSpec(memory_space=pl.ANY)] * 3,
         out_specs=whole,
         scratch_shapes=[
+            vmem(2, 2, 3, DEPTH, SLOTS), vmem(2, 2, 3, DEPTH, SLOTS), pltpu.VMEM((2, 2, DEPTH, SLOTS), jnp.int32), dma((3,)),
             vmem(ROUNDS, 4, 4, 2, 4, LANES),
             vmem(ROUNDS, 2, 2, 2, 1, LANES),
             vmem(ROUNDS, 2, 4, 4, 1, LANES),
             vmem(STEPS, size_a, 1, LANES),
             vmem(STEPS, size_b, 1, LANES),
+            vmem(16, 2, 4, LANES),
             vmem(16, 3, 3, 2, 8, LANES),
             vmem(5, 4, 8, LANES),
             vmem(16, 8, LANES),

time: 73.4 us -> 67.4 us (0.918)
  Pallas kernels: 72.7 us -> 66.6 us
    pallas_call x1, Pallas kernels: 71.9 us -> 65.9 us  [per_device(): pl.pallas_call(functools.partial(kernel, sizes), out_shape=pltpu.VMEM((10...]
where the time goes in v3:
time: 67.4 us; the launch traced here: 67.2 us
  Pallas kernels  66.6 us (99%)
    pallas_call x1, Pallas kernels, per_device(): pl.pallas_call(functools.partial(kernel, sizes), out_shape=pltpu.VMEM((10...  65.9 us

profile of v3, /device:TPU:1, one launch (start us, length us, event | category | flops | bytes accessed | tf_op | source)
XLA Modules:
  0.0 67.2 jit_solution(12523803353394620106)
XLA Ops:
  0.6 65.9 %window.1.in_ref = f32[10,8,128]{2,1,0:T(8,128)S(1)} custom-call(f32[2,2,3,8,16]{4,3,2,1,0:T(8,128)} %bitcast.6, f32[2,2,3,8,16]{4,3,2,1,0:T(8,128)} %bitcast.7, s32[2,2,8,16]{3,2,1,0:T(8,128)} %w_hbm.1), custom_call_target="tpu_custom_call" | custom-call | tf_op jit(solution)/shard_map/window/pallas_call | solution.py:336
  66.5 0.7 %unfold.1 = (f32[2,2,3,8,16]{4,3,2,1,0:T(8,128)}, f32[2,2,3,8,16]{4,3,2,1,0:T(8,128)}, f32[2,2,3,8,16]{4,3,2,1,0:T(8,128)}, f32[2,4]{1,0:T(2,128)}) custom-call(f32[10,8,128]{2,1,0:T(8,128)S(1)} %window.1.in_ref), custom_call_target="tpu_custom_call" | custom-call | tf_op jit(solution)/shard_map/unfold/pallas_call | solution.py:360

commit v4 on v3

--- a/solution.py
+++ b/solution.py
@@ -243,7 +243,7 @@
                 acc[k, c] = total[k]
             return carry
 
-        lax.fori_loop(0, 4, one_column, 0)
+        lax.fori_loop(0, 4, one_column, 0, unroll=4)
 
         sums = []
         for k in range(4):

time: 67.4 us -> 66.7 us (0.990)
  no operation moved by 1% of the time
where the time goes in v4:
time: 66.7 us; the launch traced here: 66.6 us
  Pallas kernels  66 us (99%)
    pallas_call x1, Pallas kernels, per_device(): pl.pallas_call(functools.partial(kernel, sizes), out_shape=pltpu.VMEM((10...  65.2 us

profile of v4, /device:TPU:1, one launch (start us, length us, event | category | flops | bytes accessed | tf_op | source)
XLA Modules:
  0.0 66.6 jit_solution(1752509347032939287)
XLA Ops:
  0.6 65.2 %window.1.in_ref = f32[10,8,128]{2,1,0:T(8,128)S(1)} custom-call(f32[2,2,3,8,16]{4,3,2,1,0:T(8,128)} %bitcast.6, f32[2,2,3,8,16]{4,3,2,1,0:T(8,128)} %bitcast.7, s32[2,2,8,16]{3,2,1,0:T(8,128)} %w_hbm.1), custom_call_target="tpu_custom_call" | custom-call | tf_op jit(solution)/shard_map/window/pallas_call | solution.py:336
  65.9 0.7 %unfold.1 = (f32[2,2,3,8,16]{4,3,2,1,0:T(8,128)}, f32[2,2,3,8,16]{4,3,2,1,0:T(8,128)}, f32[2,2,3,8,16]{4,3,2,1,0:T(8,128)}, f32[2,4]{1,0:T(2,128)}) custom-call(f32[10,8,128]{2,1,0:T(8,128)S(1)} %window.1.in_ref), custom_call_target="tpu_custom_call" | custom-call | tf_op jit(solution)/shard_map/unfold/pallas_call | solution.py:360

commit v5 on v4

--- a/solution.py
+++ b/solution.py
@@ -21,7 +21,8 @@
 UNIT = 2.0 ** (1.0 / 6.0)
 SIDE = CELL_SIDE / UNIT
 EDGE = FORCE_EDGE * UNIT / 12.0
-FAR = 1.0e6
+REACH = (CUTOFF / UNIT) ** 2
+FAR = 64.0
 MESH = pl.DeviceIdType.MESH
 LANES = 128
 SLOTS = 16
@@ -212,6 +213,7 @@
             for dz in (-1, 0, 1):
                 own = [jnp.broadcast_to(shifted[dz + 1, k, pl.ds(c, 1), :], (8, LANES)) for k in range(3)]
                 part = [jnp.zeros((8, LANES), jnp.float32)] * 4
+                distance = part[0]
                 for dx in (-1, 0, 1):
                     own_x = own[0] - SIDE * dx
                     for dy in (-1, 0, 1):
@@ -222,20 +224,20 @@
                             sy = expand[other, dz + 1, 1, h] - own_y
                             sz = expand[other, dz + 1, 2, h] - own[2]
                             squared = sx * sx + sy * sy + sz * sz
-                            inside = squared < (CUTOFF / UNIT) ** 2
                             if (dx, dy, dz) == (0, 0, 0):
-                                inside = inside & (slot != row + 8 * h)
-                                squared = jnp.where(inside, squared, 1.0)
+                                squared = jnp.where(slot == row + 8 * h, REACH, squared)
+                            squared = jnp.minimum(squared, REACH)
                             inverse_root = lax.rsqrt(squared)
                             inverse = inverse_root * inverse_root
                             six = inverse * inverse * inverse
                             wall = six * (six - 1.0)
-                            strength = jnp.where(inside, wall * inverse - EDGE * inverse_root, 0.0)
-                            energy = (wall - six) + (squared * inverse_root * (12.0 * EDGE) + ENERGY_SHIFT)
+                            strength = wall * inverse - EDGE * inverse_root
                             part[0] = part[0] + strength * sx
                             part[1] = part[1] + strength * sy
                             part[2] = part[2] + strength * sz
-                            part[3] = part[3] + jnp.where(inside, energy, 0.0)
+                            part[3] = part[3] + (wall - six)
+                            distance = distance + squared * inverse_root
+                part[3] = part[3] + (12.0 * EDGE) * distance + 18.0 * ENERGY_SHIFT
                 for k in range(4):
                     back = pltpu.roll(part[k], (-SLOTS * dz) % LANES, 1) if dz else part[k]
                     total[k] = back if total[k] is None else total[k] + back

time: 66.7 us -> 66.3 us (level)
  no operation moved by 1% of the time
where the time goes in v5:
time: 66.3 us; the launch traced here: 66.2 us
  Pallas kernels  65.5 us (99%)
    pallas_call x1, Pallas kernels, per_device(): pl.pallas_call(functools.partial(kernel, sizes), out_shape=pltpu.VMEM((10...  64.8 us

profile of v5, /device:TPU:1, one launch (start us, length us, event | category | flops | bytes accessed | tf_op | source)
XLA Modules:
  0.0 66.2 jit_solution(4025878021820760158)
XLA Ops:
  0.6 64.8 %window.1.in_ref = f32[10,8,128]{2,1,0:T(8,128)S(1)} custom-call(f32[2,2,3,8,16]{4,3,2,1,0:T(8,128)} %bitcast.6, f32[2,2,3,8,16]{4,3,2,1,0:T(8,128)} %bitcast.7, s32[2,2,8,16]{3,2,1,0:T(8,128)} %w_hbm.1), custom_call_target="tpu_custom_call" | custom-call | tf_op jit(solution)/shard_map/window/pallas_call | solution.py:338
  65.4 0.7 %unfold.1 = (f32[2,2,3,8,16]{4,3,2,1,0:T(8,128)}, f32[2,2,3,8,16]{4,3,2,1,0:T(8,128)}, f32[2,2,3,8,16]{4,3,2,1,0:T(8,128)}, f32[2,4]{1,0:T(2,128)}) custom-call(f32[10,8,128]{2,1,0:T(8,128)S(1)} %window.1.in_ref), custom_call_target="tpu_custom_call" | custom-call | tf_op jit(solution)/shard_map/unfold/pallas_call | solution.py:362

commit v6 on v5

--- a/solution.py
+++ b/solution.py
@@ -250,8 +250,9 @@
         sums = []
         for k in range(4):
             for c in range(4):
-                strip[c : c + 1, :] = jnp.sum(acc[k, c], axis=0, keepdims=True)
-            sums.append(jnp.where(here & (row < 4), strip[...], 0.0))
+                strip[k, c : c + 1, :] = jnp.sum(acc[k, c], axis=0, keepdims=True)
+        for k in range(4):
+            sums.append(jnp.where(here & (row < 4), strip[k], 0.0))
         force, energy = [total * (-12.0 / UNIT) for total in sums[:3]], sums[3]
         vigor = jnp.zeros((8, LANES), jnp.float32)
         for k in range(3):
@@ -352,7 +353,7 @@
             vmem(5, 4, 8, LANES),
             vmem(16, 8, LANES),
             vmem(3, 3, 8, LANES),
-            vmem(8, LANES),
+            vmem(4, 8, LANES),
             dma((ROUNDS,)), dma((ROUNDS,)), dma((ROUNDS,)), dma((ROUNDS,)),
             dma((STEPS,)), dma((STEPS,)), dma((STEPS,)), dma((STEPS,)),
         ],

time: 66.3 us -> 66.2 us (level)
  no operation moved by 1% of the time
where the time goes in v6:
time: 66.2 us; the launch traced here: 66.1 us
  Pallas kernels  65.4 us (99%)
    pallas_call x1, Pallas kernels, per_device(): pl.pallas_call(functools.partial(kernel, sizes), out_shape=pltpu.VMEM((10...  64.7 us

profile of v6, /device:TPU:1, one launch (start us, length us, event | category | flops | bytes accessed | tf_op | source)
XLA Modules:
  0.0 66.1 jit_solution(5399757864739867814)
XLA Ops:
  0.6 64.7 %window.1.in_ref = f32[10,8,128]{2,1,0:T(8,128)S(1)} custom-call(f32[2,2,3,8,16]{4,3,2,1,0:T(8,128)} %bitcast.6, f32[2,2,3,8,16]{4,3,2,1,0:T(8,128)} %bitcast.7, s32[2,2,8,16]{3,2,1,0:T(8,128)} %w_hbm.1), custom_call_target="tpu_custom_call" | custom-call | tf_op jit(solution)/shard_map/window/pallas_call | solution.py:339
  65.3 0.7 %unfold.1 = (f32[2,2,3,8,16]{4,3,2,1,0:T(8,128)}, f32[2,2,3,8,16]{4,3,2,1,0:T(8,128)}, f32[2,2,3,8,16]{4,3,2,1,0:T(8,128)}, f32[2,4]{1,0:T(2,128)}) custom-call(f32[10,8,128]{2,1,0:T(8,128)S(1)} %window.1.in_ref), custom_call_target="tpu_custom_call" | custom-call | tf_op jit(solution)/shard_map/unfold/pallas_call | solution.py:363

commit v7 on v6

--- a/solution.py
+++ b/solution.py
@@ -41,8 +41,8 @@
 
 def kernel(
     sizes, o_hbm, v_hbm, w_hbm, out_ref, o_ref, v_ref, w_ref, in_sem,
-    buf, zsrc, zbuf, red_a, red_b, lines, expand, acc, state, shifted, strip,
-    halo_recv, halo_send, z_recv, z_send, a_recv, a_send, b_recv, b_send,
+    buf, zsrc, zbuf, red_a, red_b, tally_a, tally_b, tally, lines, expand, acc, state, shifted, strip,
+    halo_recv, halo_send, z_recv, z_send, a_recv, a_send, b_recv, b_send, tally_sems,
 ):
     nx, ny, nz = sizes
     gx, gy, gz = (lax.axis_index(a) for a in ("gx", "gy", "gz"))
@@ -147,12 +147,12 @@
         for peer in group:
             pltpu.make_async_remote_copy(
                 src_ref=stage.at[k, me], dst_ref=stage.at[k, me],
-                send_sem=send_sem.at[k], recv_sem=recv_sem.at[k],
+                send_sem=send_sem, recv_sem=recv_sem,
                 device_id=peer, device_id_type=MESH,
             ).start()
 
     def collect(stage, size, recv_sem, k):
-        all_of(stage.at[k, pl.ds(0, size - 1)], recv_sem.at[k])
+        all_of(stage.at[k, pl.ds(0, size - 1)], recv_sem)
         return jnp.sum(stage[k], axis=0)
 
     def half_sum(value, width):
@@ -162,11 +162,10 @@
         return value
 
     count = jnp.sum(state[WEIGHT], axis=0, keepdims=True)
-    count = count + pltpu.roll(count, 64, 1)
-    count = count + pltpu.roll(count, 32, 1)
 
     pl.semaphore_wait(barrier, len(peers))
     ship(0)
+    share(tally_a, me_a, group_a, tally_sems.at[0], tally_sems.at[1], 0, count)
 
     def one_round(r, stretch):
         wide = jnp.broadcast_to(stretch, (8, LANES))
@@ -262,10 +261,9 @@
         @pl.when(r > 0)
         def _():
             k_row = half_sum(jnp.sum(vigor, axis=0, keepdims=True), 64)
-            u_row = half_sum(jnp.sum(energy, axis=0, keepdims=True), 32)
-            n_row = count
-            value = jnp.where(lane1 < 64, k_row, jnp.where(lane1 < 96, u_row, n_row))
-            share(red_a, me_a, group_a, a_send, a_recv, r - 1, value)
+            u_row = half_sum(jnp.sum(energy, axis=0, keepdims=True), 64)
+            value = jnp.where(lane1 < 64, k_row, u_row)
+            share(red_a, me_a, group_a, a_send.at[r - 1], a_recv.at[r - 1], r - 1, value)
 
         for k in range(3):
             state[VEL + k] = velocity[k]
@@ -277,13 +275,22 @@
         def _():
             ship(r + 1)
 
+        @pl.when(r == 0)
+        def _():
+            value = collect(tally_a, size_a, tally_sems.at[1], 0)
+            share(tally_b, me_b, group_b, tally_sems.at[2], tally_sems.at[3], 0, value)
+
+        @pl.when(r == 1)
+        def _():
+            tally[...] = jnp.broadcast_to(collect(tally_b, size_b, tally_sems.at[3], 0), (8, LANES))
+
         def reduced():
-            value = collect(red_a, size_a, a_recv, r - 1)
-            share(red_b, me_b, group_b, b_send, b_recv, r - 1, value)
-            value = collect(red_b, size_b, b_recv, r - 1)
+            value = collect(red_a, size_a, a_recv.at[r - 1], r - 1)
+            share(red_b, me_b, group_b, b_send.at[r - 1], b_recv.at[r - 1], r - 1, value)
+            value = collect(red_b, size_b, b_recv.at[r - 1], r - 1)
             vigor_sum = 0.5 * jnp.sum(jnp.where(lane1 < 64, value, 0.0), axis=1, keepdims=True)
-            body_tally = jnp.sum(jnp.where(lane1 >= 96, value, 0.0), axis=1, keepdims=True)
-            potential = 0.5 * jnp.sum(jnp.where((lane1 >= 64) & (lane1 < 96), value, 0.0), axis=1, keepdims=True)
+            body_tally = jnp.sum(tally[:1], axis=1, keepdims=True)
+            potential = 0.5 * jnp.sum(jnp.where(lane1 >= 64, value, 0.0), axis=1, keepdims=True)
             warmth = 2.0 * vigor_sum / (3.0 * body_tally)
             new = jnp.sqrt(1.0 + BATH_STRENGTH * (GOAL_WARMTH / warmth - 1.0))
             slot_total = float(nx * ny * nz * 4 * DEPTH * SLOTS)
@@ -314,6 +321,8 @@
         return carry
 
     lax.fori_loop(0, STEPS, drain_sums, 0)
+    all_of(tally_a.at[0, pl.ds(0, size_a - 1)], tally_sems.at[0])
+    all_of(tally_b.at[0, pl.ds(0, size_b - 1)], tally_sems.at[2])
 
 
 def unfold(in_ref, oo_ref, vo_ref, fo_ref, hist_ref):
@@ -348,6 +357,9 @@
             vmem(ROUNDS, 2, 4, 4, 1, LANES),
             vmem(STEPS, size_a, 1, LANES),
             vmem(STEPS, size_b, 1, LANES),
+            vmem(1, size_a, 1, LANES),
+            vmem(1, size_b, 1, LANES),
+            vmem(8, LANES),
             vmem(16, 2, 4, LANES),
             vmem(16, 3, 3, 2, 8, LANES),
             vmem(5, 4, 8, LANES),
@@ -355,7 +367,7 @@
             vmem(3, 3, 8, LANES),
             vmem(4, 8, LANES),
             dma((ROUNDS,)), dma((ROUNDS,)), dma((ROUNDS,)), dma((ROUNDS,)),
-            dma((STEPS,)), dma((STEPS,)), dma((STEPS,)), dma((STEPS,)),
+            dma((STEPS,)), dma((STEPS,)), dma((STEPS,)), dma((STEPS,)), dma((4,)),
         ],
         compiler_params=pltpu.CompilerParams(collective_id=0, has_side_effects=True),
         name="window",

time: 66.2 us -> 65.9 us (level)
  no operation moved by 1% of the time
where the time goes in v7:
time: 65.9 us; the launch traced here: 65.8 us
  Pallas kernels  65.2 us (99%)
    pallas_call x1, Pallas kernels, per_device(): pl.pallas_call(functools.partial(kernel, sizes), out_shape=pltpu.VMEM((10...  64.4 us

profile of v7, /device:TPU:1, one launch (start us, length us, event | category | flops | bytes accessed | tf_op | source)
XLA Modules:
  0.0 65.8 jit_solution(2466199404980680455)
XLA Ops:
  0.6 64.4 %window.1.in_ref = f32[10,8,128]{2,1,0:T(8,128)S(1)} custom-call(f32[2,2,3,8,16]{4,3,2,1,0:T(8,128)} %bitcast.6, f32[2,2,3,8,16]{4,3,2,1,0:T(8,128)} %bitcast.7, s32[2,2,8,16]{3,2,1,0:T(8,128)} %w_hbm.1), custom_call_target="tpu_custom_call" | custom-call | tf_op jit(solution)/shard_map/window/pallas_call | solution.py:348
  65.1 0.7 %unfold.1 = (f32[2,2,3,8,16]{4,3,2,1,0:T(8,128)}, f32[2,2,3,8,16]{4,3,2,1,0:T(8,128)}, f32[2,2,3,8,16]{4,3,2,1,0:T(8,128)}, f32[2,4]{1,0:T(2,128)}) custom-call(f32[10,8,128]{2,1,0:T(8,128)S(1)} %window.1.in_ref), custom_call_target="tpu_custom_call" | custom-call | tf_op jit(solution)/shard_map/unfold/pallas_call | solution.py:375

commit v8 on v7

--- a/solution.py
+++ b/solution.py
@@ -54,12 +54,12 @@
 
     group_a = [
         (gx, high * 2 + lax.rem(core + dc, 2), lax.rem(gz + dz, nz))
-        for dz in range(nz) for dc in range(2) if (dz, dc) != (0, 0)
+        for dz in sorted(range(nz), key=lambda d: -min(d, nz - d)) for dc in (1, 0) if (dz, dc) != (0, 0)
     ]
     me_a = gz * 2 + core
     group_b = [
         (lax.rem(gx + dx, nx), lax.rem(high + dh, n_high) * 2 + core, gz)
-        for dx in range(nx) for dh in range(n_high) if (dx, dh) != (0, 0)
+        for dx in sorted(range(nx), key=lambda d: -min(d % 4, 4 - d % 4)) for dh in reversed(range(n_high)) if (dx, dh) != (0, 0)
     ]
     me_b = gx * n_high + high
     size_a, size_b = nz * 2, nx * n_high

time: 65.9 us -> 65.4 us (level)
  no operation moved by 1% of the time
where the time goes in v8:
time: 65.4 us; the launch traced here: 65.2 us
  Pallas kernels  64.6 us (99%)
    pallas_call x1, Pallas kernels, per_device(): pl.pallas_call(functools.partial(kernel, sizes), out_shape=pltpu.VMEM((10...  63.8 us

profile of v8, /device:TPU:1, one launch (start us, length us, event | category | flops | bytes accessed | tf_op | source)
XLA Modules:
  0.0 65.2 jit_solution(15860839328033708560)
XLA Ops:
  0.6 63.8 %window.1.in_ref = f32[10,8,128]{2,1,0:T(8,128)S(1)} custom-call(f32[2,2,3,8,16]{4,3,2,1,0:T(8,128)} %bitcast.6, f32[2,2,3,8,16]{4,3,2,1,0:T(8,128)} %bitcast.7, s32[2,2,8,16]{3,2,1,0:T(8,128)} %w_hbm.1), custom_call_target="tpu_custom_call" | custom-call | tf_op jit(solution)/shard_map/window/pallas_call | solution.py:348
  64.5 0.7 %unfold.1 = (f32[2,2,3,8,16]{4,3,2,1,0:T(8,128)}, f32[2,2,3,8,16]{4,3,2,1,0:T(8,128)}, f32[2,2,3,8,16]{4,3,2,1,0:T(8,128)}, f32[2,4]{1,0:T(2,128)}) custom-call(f32[10,8,128]{2,1,0:T(8,128)S(1)} %window.1.in_ref), custom_call_target="tpu_custom_call" | custom-call | tf_op jit(solution)/shard_map/unfold/pallas_call | solution.py:375
